TPU v7x, 32 devices: a whole 2x2x4 slice. The times are simulated.
32 devices in a mesh: depth: 8 (over z, x), rows: 4 (over y, core).
Axes of the slice: x: 2, y: 2, z: 4, core: 2. Of those that a mesh axis runs over, the one named last changes fastest.
Arguments:
- density: float32 [128, 64, 1024], P('depth', 'rows'), may hold values from 0 to 1
- bin_of_level: int32 [16], replicated, may hold values from 0 to 7
- absorb_bins: float32 [8], replicated, may hold values from 0.00234375 to 0.0625
- emit_bins: float32 [8], replicated, may hold values from 0.2 to 3
- occupancy: int32 [8, 4, 8], P('depth', 'rows'), may hold values 0 or 1
- col_offsets: int32 [1024], replicated, may hold values from 2 to 6
- row_offsets: int32 [64], P('rows'), may hold values from 2 to 6
Outputs:
- front_transmittance: float32 [8, 64, 1024], P('depth', 'rows')
- final_image: float32 [2, 64, 1024], P(None, 'rows')
All inputs are finite; a program needn't handle non-finite values. No bound on the sum of `occupancy` on one device may be relied on, other than what follows from the above.
Results may differ from a plain program's by a relative error of at most 0.0002.
Values sent between devices are 32-bit elements; how exact they have to be, the bound alone decides.
No kernel may reach another device: no remote copies, remote signals or barrier semaphores. Data moves between devices by JAX's collectives and lax.ppermute only.
A program may use at most 64 MiB of HBM per device.

v0:
```python
import jax
import jax.numpy as jnp
from jax import lax
from jax.sharding import PartitionSpec as P


def from_behind(block, axis, distance):
    devices = range(lax.axis_size(axis))
    route = [(i - distance, i) for i in devices if i - distance in devices]
    return lax.ppermute(block, axis, route)


def resample_columns(mixed, col_offsets):
    fraction = col_offsets.astype(jnp.float32) / 8.0
    pad_shape = mixed.shape[:-1] + (1,)
    right_side = jnp.concatenate([mixed[..., 1:], jnp.zeros(pad_shape, jnp.float32)], -1)
    return (1.0 - fraction) * mixed + fraction * right_side


def tables(bin_of_level, absorb_bins, emit_bins):
    count_bins = absorb_bins.shape[0]
    onehot = (bin_of_level[:, None] == jnp.arange(count_bins, dtype=jnp.int32)[None, :]).astype(
        jnp.float32
    )
    return (jnp.sum(onehot * absorb_bins[None, :], 1), jnp.sum(onehot * emit_bins[None, :], 1))


def classify(sampled, absorb_level, emit_level):
    levels = absorb_level.shape[0]
    scaled = sampled * float(levels - 1)
    absorption = jnp.zeros(sampled.shape, jnp.float32)
    emission = jnp.zeros(sampled.shape, jnp.float32)
    for knot_index in range(levels):
        weight = jnp.maximum(0.0, 1.0 - jnp.abs(scaled - float(knot_index)))
        absorption = absorption + weight * absorb_level[knot_index]
        emission = emission + weight * emit_level[knot_index]
    return (absorption, emission)


def composite(absorption, emission):
    inclusive = jnp.cumsum(absorption, 0)
    exclusive = inclusive - absorption
    light = jnp.sum(jnp.exp(-exclusive) * (1.0 - jnp.exp(-absorption)) * emission, 0)
    return (light, inclusive[-1])


def on_device(density, bin_of_level, absorb_bins, emit_bins, occupancy, col_offsets, row_offsets):
    following = from_behind(density[:1], "depth", -1)
    extended = jnp.concatenate([density, following], 0)
    mid_depth = 0.5 * (extended[:-1] + extended[1:])
    row_below = from_behind(mid_depth[:, :1], "rows", -1)
    next_rows = jnp.concatenate([mid_depth[:, 1:], row_below], 1)
    frac_row = (row_offsets.astype(jnp.float32) / 8.0)[None, :, None]
    mixed = (1.0 - frac_row) * mid_depth + frac_row * next_rows
    sampled = resample_columns(mixed, col_offsets)
    absorb_level, emit_level = tables(bin_of_level, absorb_bins, emit_bins)
    occupied = occupancy[0, 0]
    absorption, emission = classify(sampled, absorb_level, emit_level)
    brick_mask = jnp.repeat(occupied.astype(jnp.float32), 128)
    absorption = absorption * brick_mask[None, None, :]
    light, depth_sum = composite(absorption, emission)
    position = lax.axis_index("depth")
    pieces = lax.all_gather(depth_sum[None], "depth", axis=0, tiled=True)
    shard_ids = jnp.arange(pieces.shape[0], dtype=jnp.int32)
    in_front = (shard_ids < position)[:, None, None]
    front_depth = jnp.sum(jnp.where(in_front, pieces, 0.0), 0)
    total_depth = jnp.sum(pieces, 0)
    front = jnp.exp(-front_depth)
    radiance = lax.psum(front * light, "depth")
    final_image = jnp.stack([radiance, jnp.exp(-total_depth)])
    return (front[None], final_image)


def solution(mesh):
    placed = (P("depth", "rows", None), P(), P(), P(), P("depth", "rows", None), P(), P("rows"))
    return jax.shard_map(
        on_device,
        mesh=mesh,
        in_specs=placed,
        out_specs=(P("depth", "rows", None), P(None, "rows", None)),
        check_vma=False,
    )
```

profile of v0, /device:TPU:0, one launch (start us, length us, event | category | flops | bytes accessed | tf_op | source)
XLA Modules:
  0.0 160.8 jit_solution(6802575559535258758)
XLA Ops:
  7.2 0.0 all-reduce.3.cloned.1.call-start
  7.2 0.8 slice.114
  8.1 0.0 copy-start.2
  8.1 0.0 copy-start.3
  8.1 0.0 copy-start.4
  8.1 1.4 collective-permute-start
  9.5 0.0 copy-done.2
  9.5 0.0 copy-done.3
  9.5 0.0 copy-done.4
  9.5 0.1 select_reduce_fusion.1
  9.6 0.0 copy-start.5
  9.6 0.0 copy-start.1
  9.6 0.7 fusion.59
  10.4 0.0 copy-done.5
  10.4 0.0 copy-done.1
  10.4 0.0 copy-start.6
  10.4 0.6 copy-done.6
  11.1 0.1 broadcast_bitcast_fusion
  11.1 0.7 fusion.58
  11.8 3.5 %collective-permute-done = f32[1,16,1024]{2,1,0:T(8,128)S(1)} collective-permute-done((f32[1,16,1024]{2,1,0:T(8,128)S(1)}, f32[1,16,1024]{2,1,0:T(8,128)S(1)}, u32[]{:S(2)}, u32[]{:S(2)}) %collective-permute-start) | collective-permute-done | bytes 65568 | tf_op jit(solution)/shard_map/ppermute | solution.py:10
  15.3 1.7 %fusion.3 = f32[16,16,1024]{2,1,0:T(8,128)S(1)} fusion(f32[16,16,1024]{2,1,0:T(8,128)} %param.7, f32[1,16,1024]{2,1,0:T(8,128)S(1)} %collective-permute-done), kind=kLoop, calls=%fused_computation.24 | loop fusion | flops 786432 | bytes 2162688 | tf_op jit(solution)/shard_map/mul | solution.py:50
  17.1 1.3 collective-permute-start.1
  18.4 0.0 copy-start
  18.4 0.1 slice.152
  18.6 1.7 %collective-permute-done.1 = f32[16,1,1024]{2,1,0:T(1,128)S(1)} collective-permute-done((f32[16,1,1024]{2,1,0:T(1,128)S(1)}, f32[16,1,1024]{2,1,0:T(1,128)S(1)}, u32[]{:S(2)}, u32[]{:S(2)}) %collective-permute-start.1) | collective-permute-done | bytes 65568 | tf_op jit(solution)/shard_map/ppermute | solution.py:10
  20.3 0.0 copy-done
  20.3 0.3 fusion.1
  20.6 0.3 slice.154
  21.0 28.9 %multiply_reduce_fusion = (f32[16,1024]{1,0:T(8,128)S(1)}, f32[16,16,1024]{2,1,0:T(8,128)S(1)}) fusion(f32[]{:T(128)} %bitcast.34, f32[]{:T(128)} %bitcast.33, f32[]{:T(128)} %bitcast.32, f32[]{:T(128)} %bitcast.31, f32[]{:T(128)} %bitcast.30, f32[]{:T(128)} %bitcast.29, f32[]{:T(128)} %bitcast.28, f32[]{:T(128)} %bitcast.27, f32[]{:T(128)} %bitcast.26, ...), kind=kOutput, calls=%fused_computation.4 | output fusion | flops 65781760 | bytes 3222656 | tf_op jit(solution)/shard_map/jit(cumsum)/reduce_window_sum | solution.py:41
  49.8 32.2 %all_gather.3 = f32[8,16,1024]{2,1,0:T(8,128)S(1)} all-gather(f32[1,16,1024]{2,1,0:T(8,128)S(1)} %slice.155), channel_id=1, replica_groups=mesh['depth'=8,'rows'=4] {'depth'}, dimensions={0}, use_global_device_ids=true | all-gather | bytes 589824 | tf_op jit(solution)/shard_map/all_gather | solution.py:63
  82.0 0.1 fusion.57
  82.1 0.7 multiply_bitcast_fusion
  82.8 0.0 all-reduce.3.cloned.1.call-update
  82.8 69.7 %all-reduce.3.cloned.1.call-done = f32[1,16,1024]{2,1,0:T(8,128)} async-done(((f32[1,16,1024]{2,1,0:T(8,128)}), f32[1,16,1024]{2,1,0:T(8,128)}) %all-reduce.3.cloned.1.call-update) | async-done | bytes 65552 | tf_op jit(solution)/shard_map/psum | solution.py:69
  152.5 1.5 pad_maximum_fusion.1
  (7 shorter events, 0.1 us)
Async XLA Ops:
  7.2 145.3 %all-reduce.3.cloned.1.call-start = ((), (), s32[]{:S(2)}) async-start(), calls=%async_computation | async-start | bytes 131072 | tf_op jit(solution)/shard_map/psum | solution.py:69
  8.1 1.5 copy-start.2
  8.1 1.5 copy-start.3
  8.1 1.5 copy-start.4
  8.1 7.2 %collective-permute-start = (f32[1,16,1024]{2,1,0:T(8,128)S(1)}, f32[1,16,1024]{2,1,0:T(8,128)S(1)}, u32[]{:S(2)}, u32[]{:S(2)}) collective-permute-start(f32[1,16,1024]{2,1,0:T(8,128)S(1)} %slice.114), channel_id=1, source_target_pairs={{4,0},{8,4},{12,8},{16,12},{20,16},{24,20},{28,24},{5,1},{9,5},{13... | collective-permute-start | bytes 196616 | tf_op jit(solution)/shard_map/ppermute | solution.py:10
  9.6 0.7 copy-start.5
  9.6 0.8 copy-start.1
  10.4 0.7 copy-start.6
  17.1 3.1 %collective-permute-start.1 = (f32[16,1,1024]{2,1,0:T(1,128)S(1)}, f32[16,1,1024]{2,1,0:T(1,128)S(1)}, u32[]{:S(2)}, u32[]{:S(2)}) collective-permute-start(f32[16,1,1024]{2,1,0:T(1,128)S(1)} %slice.153), channel_id=1, source_target_pairs={{1,0},{2,1},{3,2},{5,4},{6,5},{7,6},{9,8},{10,9},{11,10},{13,12},{... | collective-permute-start | bytes 196616 | tf_op jit(solution)/shard_map/ppermute | solution.py:10
  18.4 1.8 %copy-start = (f32[16,16,1024]{2,1,0:T(8,128)S(1)}, f32[16,16,1024]{2,1,0:T(8,128)}, u32[]{:S(2)}) copy-start(f32[16,16,1024]{2,1,0:T(8,128)} %param.7) | copy-start | bytes 3145732
Sparse Core Ops, SparseCore 0:
  82.9 69.5 all-reduce.2
where the time goes:
time: 161 us
  waiting for transfers between devices  74.8 us (46%)
  other arithmetic  33.3 us (21%)
  blocking collectives  32.2 us (20%)
  between operations  14.2 us (9%)
  local copies, waits for them, and re-layouts  3.52 us (2%)
  starting transfers between devices  2.75 us (2%)
    psum x1, waiting for transfers between devices, on_device(): radiance = lax.psum(front * light, 'depth')  69.7 us
    all_gather x1, blocking collectives, on_device(): pieces = lax.all_gather(depth_sum[None], 'depth', axis=0, tiled=True)  32.2 us
    another operation x1, other arithmetic, composite(): inclusive = jnp.cumsum(absorption, 0)  28.9 us
    ppermute x2, waiting for transfers between devices, from_behind(): return lax.ppermute(block, axis, route)  5.18 us
  transfers between devices with their start and end apart: 3, of which 3 were waited for; matrix products, arithmetic and copies ran while one was open for 1% of the time, Pallas kernels for 0%

commit v1 on v0

v1 whole, which is shorter than its diff:
```python
import functools
import math

import jax
import jax.numpy as jnp
from jax import lax
from jax.experimental import pallas as pl
from jax.experimental.pallas import tpu as pltpu
from jax.sharding import PartitionSpec as P

WIDTH = 256


def from_behind(block, axis):
    size = lax.axis_size(axis)
    return lax.ppermute(block, axis, [(i + 1, i) for i in range(size - 1)])


def from_diagonal(block):
    depth, rows = lax.axis_size("depth"), lax.axis_size("rows")
    route = [
        ((z + 1) * rows + y + 1, z * rows + y)
        for z in range(depth - 1)
        for y in range(rows - 1)
    ]
    return lax.ppermute(block, ("depth", "rows"), route)


def tables(bin_of_level, absorb_bins, emit_bins):
    count_bins = absorb_bins.shape[0]
    onehot = bin_of_level[:, None] == jnp.arange(count_bins, dtype=jnp.int32)[None, :]

    def coefficients(bins):
        level = jnp.sum(jnp.where(onehot, bins[None, :], 0.0), 1)
        slope = level[1:] - level[:-1]
        gain = jnp.concatenate([slope[:1], slope[1:] - slope[:-1]])
        knots = jnp.arange(gain.shape[0], dtype=jnp.float32)
        base = level[0] - jnp.sum(gain * knots)
        rows = jnp.concatenate([base[None], gain])
        return jnp.broadcast_to(rows[:, None], (rows.shape[0], 128))

    return coefficients(absorb_bins * (-1.0 / math.log(2.0))), coefficients(emit_bins)


def render(density, plane, row, corner, weights, fraction, occupied, absorb, emit, state, scaled):
    planes, rows, cols = density.shape
    levels = absorb.shape[0]
    last_row = lax.broadcasted_iota(jnp.int32, (rows, 128), 0) == rows - 1
    last_lane = lax.broadcasted_iota(jnp.int32, (rows, 128), 1) == 127
    near, far = weights[0], weights[1]

    @pl.loop(0, planes)
    def _(z):
        last = z == planes - 1
        after = jnp.minimum(z + 1, planes - 1)

        def mixed(tile):
            at = pl.ds(tile * 128, 128)
            behind = jnp.where(last, plane[0, :, at], density[after, :, at])
            mid = density[z, :, at] + behind
            below = row[z, :, at] + jnp.where(last, corner[0, :, at], row[after, :, at])
            shifted = jnp.where(last_row, below, pltpu.roll(mid, rows - 1, 0))
            return near * mid + far * shifted

        current = mixed(0)
        rolled = pltpu.roll(current, 127, 1)
        tiles = cols // 128
        for tile in range(tiles):
            if tile + 1 < tiles:
                following = mixed(tile + 1)
                following_rolled = pltpu.roll(following, 127, 1)
                right = jnp.where(last_lane, following_rolled, rolled)
            else:
                right = jnp.where(last_lane, 0.0, rolled)
            part = fraction[tile : tile + 1, :]
            scaled[z, :, pl.ds(tile * 128, 128)] = (1.0 - part) * current + part * right
            if tile + 1 < tiles:
                current, rolled = following, following_rolled

    @pl.loop(0, cols // WIDTH)
    def _(tile):
        at = pl.ds(pl.multiple_of(tile * WIDTH, WIDTH), WIDTH)
        shape = (rows, WIDTH)
        mask = jnp.concatenate(
            [
                jnp.broadcast_to(occupied[pl.ds(tile * (WIDTH // 128) + i, 1), :], (rows, 128))
                for i in range(WIDTH // 128)
            ],
            1,
        )

        def splat(ref, k):
            return jnp.broadcast_to(jnp.concatenate([ref[k : k + 1, :]] * (WIDTH // 128), 1), shape)

        total = jnp.zeros(shape, jnp.float32)
        through = jnp.ones(shape, jnp.float32)
        light = jnp.zeros(shape, jnp.float32)
        for z in range(planes):
            value = scaled[z, :, at]
            absorption = splat(absorb, 0) + splat(absorb, 1) * value
            emission = splat(emit, 0) + splat(emit, 1) * value
            for k in range(1, levels - 1):
                kink = jnp.maximum(value, float(k))
                absorption += splat(absorb, k + 1) * kink
                emission += splat(emit, k + 1) * kink
            total += absorption * mask
            behind = jnp.exp2(total)
            light += (through - behind) * emission
            through = behind
        state[0, :, at] = light
        state[1, :, at] = through


def on_device(density, bin_of_level, absorb_bins, emit_bins, occupancy, col_offsets, row_offsets):
    planes, rows, cols = density.shape
    plane = from_behind(density[:1], "depth")
    row = from_behind(density[:, :1], "rows")
    corner = from_diagonal(density[:1, :1])
    absorb, emit = tables(bin_of_level, absorb_bins, emit_bins)
    levels = bin_of_level.shape[0]
    frac_row = row_offsets.astype(jnp.float32) / 8.0
    scale = 0.5 * (levels - 1)
    weights = jnp.broadcast_to(
        scale * jnp.stack([1.0 - frac_row, frac_row])[:, :, None], (2, rows, 128)
    )
    fraction = (col_offsets.astype(jnp.float32) / 8.0).reshape(cols // 128, 128)
    occupied = jnp.broadcast_to(
        occupancy[0, 0].astype(jnp.float32)[:, None], (cols // 128, 128)
    )
    vmem = pl.BlockSpec(memory_space=pltpu.VMEM)
    state = pl.pallas_call(
        render,
        out_shape=jax.ShapeDtypeStruct((2, rows, cols), jnp.float32),
        in_specs=[vmem] * 9,
        out_specs=vmem,
        scratch_shapes=[pltpu.VMEM((planes, rows, cols), jnp.float32)],
        cost_estimate=pl.CostEstimate(
            flops=100 * density.size, bytes_accessed=4 * density.size, transcendentals=density.size
        ),
        name="render",
    )(density, plane, row, corner, weights, fraction, occupied, absorb, emit)

    size = lax.axis_size("depth")
    position = lax.axis_index("depth")
    front = jnp.ones((1, rows, cols), jnp.float32)
    step = 1
    while step < size:
        other = lax.ppermute(state, "depth", [(i, i ^ step) for i in range(size)])
        behind = (position & step) != 0
        first = jnp.where(behind, other, state)
        second = jnp.where(behind, state, other)
        front = front * jnp.where(behind, other[1:], 1.0)
        state = jnp.stack([first[0] + first[1] * second[0], first[1] * second[1]])
        step *= 2
    return (front, state)


def solution(mesh):
    placed = (P("depth", "rows", None), P(), P(), P(), P("depth", "rows", None), P(), P("rows"))
    return jax.shard_map(
        on_device,
        mesh=mesh,
        in_specs=placed,
        out_specs=(P("depth", "rows", None), P(None, "rows", None)),
        check_vma=False,
    )
```

time: 161 us -> 48.5 us (0.30)
  waiting for transfers between devices: 74.8 us -> 14.1 us
  blocking collectives: 32.2 us -> 0 us
  other arithmetic: 33.3 us -> 4.9 us
  between operations: 14.2 us -> 2.2 us
  starting transfers between devices: 2.75 us -> 14 us
  Pallas kernels: 0 us -> 6.33 us
  local copies, waits for them, and re-layouts: 3.52 us -> 6.6 us
    psum x1 -> x0, waiting for transfers between devices: 69.7 us -> none  [on_device(): radiance = lax.psum(front * light, 'depth')]
    all_gather x1 -> x0, blocking collectives: 32.2 us -> none  [on_device(): pieces = lax.all_gather(depth_sum[None], 'depth', axis=0, tiled=True)]
    another operation x3 -> x4, other arithmetic: 31 us -> 0.69 us  [the longest x3 0.69 us: on_device(): state = jnp.stack([first[0] + first[1] * second[0], first[1] * second[1]])]
    ppermute x2 -> x6, starting transfers between devices: 2.72 us -> 14 us  [the longest x3 9.98 us: on_device(): other = lax.ppermute(state, 'depth', [(i, i ^ step) for i in range(size)])]
    ppermute x2 -> x6, waiting for transfers between devices: 5.18 us -> 14.1 us  [the longest x3 14.1 us: on_device(): other = lax.ppermute(state, 'depth', [(i, i ^ step) for i in range(size)])]
    pallas_call x0 -> x1, Pallas kernels: none -> 6.33 us  [on_device(): pl.pallas_call(render, out_shape=jax.ShapeDtypeStruct((2, rows, cols), jn...]
    broadcast_in_dim x0 -> x4, local copies, waits for them, and re-layouts: none -> 2.65 us  [the longest x2 1.33 us: coefficients(): return jnp.broadcast_to(rows[:, None], (rows.shape[0], 128))]
  transfers between devices with their start and end apart: 3 -> 6, of which waited for: 3 -> 3; matrix products, arithmetic and copies ran while one was open for 1% -> 9% of each run, Pallas kernels for 0% -> 0%
where the time goes in v1:
time: 48.5 us; the launch traced here: 48.1 us
  waiting for transfers between devices  14.1 us (29%)
  starting transfers between devices  14 us (29%)
  local copies, waits for them, and re-layouts  6.6 us (14%)
  Pallas kernels  6.33 us (13%)
  other arithmetic  4.9 us (10%)
  between operations  2.2 us (5%)
    ppermute x3, waiting for transfers between devices, on_device(): other = lax.ppermute(state, 'depth', [(i, i ^ step) for i in range(size)])  14.1 us
    ppermute x3, starting transfers between devices, on_device(): other = lax.ppermute(state, 'depth', [(i, i ^ step) for i in range(size)])  9.98 us
    pallas_call x1, Pallas kernels, on_device(): pl.pallas_call(render, out_shape=jax.ShapeDtypeStruct((2, rows, cols), jn...  6.33 us
    ppermute x2, starting transfers between devices, from_behind(): return lax.ppermute(block, axis, [(i + 1, i) for i in range(size - 1)])  2.7 us
    reduce_sum x2, other arithmetic, coefficients(): base = level[0] - jnp.sum(gain * knots)  1.41 us
    broadcast_in_dim x2, local copies, waits for them, and re-layouts, coefficients(): return jnp.broadcast_to(rows[:, None], (rows.shape[0], 128))  1.33 us
    ppermute x1, starting transfers between devices, from_diagonal(): return lax.ppermute(block, ('depth', 'rows'), route)  1.28 us
    unnamed x18, local copies, waits for them, and re-layouts  1.26 us
  transfers between devices with their start and end apart: 6, of which 3 were waited for; matrix products, arithmetic and copies ran while one was open for 9% of the time, Pallas kernels for 0%

profile of v1, /device:TPU:0, one launch (start us, length us, event | category | flops | bytes accessed | tf_op | source)
XLA Modules:
  0.0 48.1 jit_solution(5988678999158183055)
XLA Ops:
  0.6 0.8 %slice.95 = f32[1,1,1024]{2,1,0:T(1,128)S(1)} slice(f32[16,16,1024]{2,1,0:T(8,128)} %density.1), slice={[0:1], [0:1], [0:1024]} | slice | bytes 8192 | tf_op jit(solution)/shard_map/slice | solution.py:118
  1.4 1.3 %collective-permute-start.2 = (f32[1,1,1024]{2,1,0:T(1,128)S(1)}, f32[1,1,1024]{2,1,0:T(1,128)S(1)}, u32[]{:S(2)}, u32[]{:S(2)}) collective-permute-start(f32[1,1,1024]{2,1,0:T(1,128)S(1)} %slice.95), channel_id=1, source_target_pairs={{5,0},{6,1},{7,2},{9,4},{10,5},{11,6},{13,8},{14,9},{15,10},{17,12... | collective-permute-start | bytes 12296 | tf_op jit(solution)/shard_map/ppermute | solution.py:26
  2.7 0.8 %slice.93 = f32[1,16,1024]{2,1,0:T(8,128)S(1)} slice(f32[16,16,1024]{2,1,0:T(8,128)} %density.1), slice={[0:1], [0:16], [0:1024]} | slice | bytes 131072 | tf_op jit(solution)/shard_map/slice | solution.py:116
  3.5 0.0 copy-start.6
  3.5 1.4 %collective-permute-start = (f32[1,16,1024]{2,1,0:T(8,128)S(1)}, f32[1,16,1024]{2,1,0:T(8,128)S(1)}, u32[]{:S(2)}, u32[]{:S(2)}) collective-permute-start(f32[1,16,1024]{2,1,0:T(8,128)S(1)} %slice.93), channel_id=1, source_target_pairs={{4,0},{8,4},{12,8},{16,12},{20,16},{24,20},{28,24},{5,1},{9,5},{13... | collective-permute-start | bytes 196616 | tf_op jit(solution)/shard_map/ppermute | solution.py:16
  4.9 1.1 %slice.94 = f32[16,1,1024]{2,1,0:T(1,128)S(1)} slice(f32[16,16,1024]{2,1,0:T(8,128)} %density.1), slice={[0:16], [0:1], [0:1024]} | slice | bytes 131072 | tf_op jit(solution)/shard_map/slice | solution.py:117
  6.0 0.0 copy-start.7
  6.0 1.3 %collective-permute-start.1 = (f32[16,1,1024]{2,1,0:T(1,128)S(1)}, f32[16,1,1024]{2,1,0:T(1,128)S(1)}, u32[]{:S(2)}, u32[]{:S(2)}) collective-permute-start(f32[16,1,1024]{2,1,0:T(1,128)S(1)} %slice.94), channel_id=1, source_target_pairs={{1,0},{2,1},{3,2},{5,4},{6,5},{7,6},{9,8},{10,9},{11,10},{13,12},{... | collective-permute-start | bytes 196616 | tf_op jit(solution)/shard_map/ppermute | solution.py:16
  7.3 0.0 copy-done.6
  7.4 0.0 copy-done.7
  7.4 0.0 copy-start.4
  7.4 0.0 copy-start.5
  7.4 0.6 %copy-done.4 = f32[8]{0:T(128)S(1)} copy-done((f32[8]{0:T(128)S(1)}, f32[8]{0:T(128)}, u32[]{:S(2)}) %copy-start.4) | copy-done | bytes 56
  8.0 0.0 copy-done.5
  8.0 0.1 select_reduce_fusion
  8.1 0.1 slice_subtract_fusion.1
  8.2 0.1 slice_subtract_fusion
  8.3 0.7 %fusion.6 = f32[]{:T(128)} fusion(f32[14]{0:T(128)S(1)} %slice_subtract_fusion, f32[1]{0:T(128)S(1)} %bitcast.20), kind=kLoop, calls=%fused_computation.32 | loop fusion | flops 44 | bytes 64 | tf_op jit(solution)/shard_map/reduce_sum | solution.py:38
  9.7 0.0 copy-start.3
  9.7 0.1 pad_maximum_fusion.4
  9.8 0.1 slice_subtract_fusion.2
  9.9 0.6 %copy-done.8 = s32[16]{0:T(128)S(1)} copy-done((s32[16]{0:T(128)S(1)}, s32[16]{0:T(128)}, u32[]{:S(2)}) %copy-start.8) | copy-done | bytes 88
  10.5 0.0 copy-done.3
  10.5 0.6 %multiply_bitcast_fusion.fraction = f32[8,128]{1,0:T(8,128)} fusion(s32[1024]{0:T(1024)S(1)} %copy-done.3), kind=kLoop, calls=%fused_computation.26 | loop fusion | flops 2048 | bytes 8192 | tf_op jit(solution)/shard_map/reshape | solution.py:126
  11.1 0.7 %fusion.5 = f32[]{:T(128)} fusion(f32[14]{0:T(128)S(1)} %slice_subtract_fusion.2, f32[1]{0:T(128)S(1)} %bitcast.18), kind=kLoop, calls=%fused_computation.29 | loop fusion | flops 44 | bytes 64 | tf_op jit(solution)/shard_map/reduce_sum | solution.py:38
  12.5 0.1 pad_maximum_fusion.3
  12.6 0.0 collective-permute-done.2.corner
  12.6 0.0 collective-permute-done.plane
  12.6 0.0 copy-start
  12.6 0.0 collective-permute-done.1.row
  12.6 0.0 copy-start.1
  12.6 0.7 %broadcast_in_dim.59.occupied = f32[8,128]{1,0:T(8,128)} broadcast(f32[8]{0:T(128)S(1)} %convert_bitcast_fusion), dimensions={0} | broadcast | bytes 4128 | tf_op jit(solution)/shard_map/broadcast_in_dim | solution.py:127
  13.3 0.7 %broadcast_in_dim.63.absorb = f32[16,128]{1,0:T(8,128)} broadcast(f32[16]{0:T(128)S(1)} %pad_maximum_fusion.3), dimensions={0} | broadcast | bytes 8256 | tf_op jit(solution)/shard_map/broadcast_in_dim | solution.py:40
  14.0 0.0 copy-done.2
  14.0 0.7 %broadcast_in_dim.66.emit = f32[16,128]{1,0:T(8,128)} broadcast(f32[16]{0:T(128)S(1)} %pad_maximum_fusion.4), dimensions={0} | broadcast | bytes 8256 | tf_op jit(solution)/shard_map/broadcast_in_dim | solution.py:40
  14.6 0.7 %broadcast_in_dim.58.weights = f32[2,16,128]{2,1,0:T(8,128)} broadcast(f32[2,16]{1,0:T(2,128)S(1)} %maximum_multiply_fusion), dimensions={0,1} | broadcast | bytes 16512 | tf_op jit(solution)/shard_map/broadcast_in_dim | solution.py:123
  15.3 0.0 copy-done
  15.3 0.0 copy-done.1
  15.3 6.3 %render.1 = f32[2,16,1024]{2,1,0:T(8,128)} custom-call(f32[16,16,1024]{2,1,0:T(8,128)} %density.1, f32[1,16,1024]{2,1,0:T(8,128)} %copy-done, f32[16,1,1024]{2,1,0:T(1,128)} %copy-done.1, f32[1,1,1024]{2,1,0:T(1,128)} %copy-done.2, f32[2,16,128]{2,1,0:T(8,128)} %broadcast_in_dim.58.weights, f32[8,128]{1,0:T(8,128)} %multiply_bitcast_fusion.fraction, ...), custom_call_target="tpu_custom_call" | custom-call | flops 26214400 | bytes 1048576 | tf_op jit(solution)/shard_map/render/pallas_call | solution.py:131
  21.6 3.6 %collective-permute-start.3 = (f32[2,16,1024]{2,1,0:T(8,128)}, f32[2,16,1024]{2,1,0:T(8,128)S(1)}, u32[]{:S(2)}, u32[]{:S(2)}) collective-permute-start(f32[2,16,1024]{2,1,0:T(8,128)} %render.1), channel_id=1, source_target_pairs={{0,4},{4,0},{8,12},{12,8},{16,20},{20,16},{24,28},{28,24},{1,5},{5... | collective-permute-start | bytes 393224 | tf_op jit(solution)/shard_map/ppermute | solution.py:148
  25.2 4.1 %collective-permute-done.3 = f32[2,16,1024]{2,1,0:T(8,128)S(1)} collective-permute-done((f32[2,16,1024]{2,1,0:T(8,128)}, f32[2,16,1024]{2,1,0:T(8,128)S(1)}, u32[]{:S(2)}, u32[]{:S(2)}) %collective-permute-start.3) | collective-permute-done | bytes 131104 | tf_op jit(solution)/shard_map/ppermute | solution.py:148
  29.3 0.9 %broadcast_select_fusion.5 = (f32[2,16,1024]{2,1,0:T(8,128)S(1)}, f32[2,16,1024]{2,1,0:T(8,128)S(1)}) fusion(f32[2,16,1024]{2,1,0:T(8,128)S(1)} %collective-permute-done.3, f32[2,16,1024]{2,1,0:T(8,128)} %render.1, pred[]{:T(512)S(6)} %ne.9), kind=kLoop, calls=%fused_computation.22 | loop fusion | flops 65536 | bytes 524289 | tf_op jit(solution)/shard_map/jit(_where)/select_n | solution.py:150
  30.3 3.6 %collective-permute-start.4 = (f32[2,16,1024]{2,1,0:T(8,128)S(1)}, f32[2,16,1024]{2,1,0:T(8,128)S(1)}, u32[]{:S(2)}, u32[]{:S(2)}) collective-permute-start(f32[2,16,1024]{2,1,0:T(8,128)S(1)} %pad_maximum_fusion), channel_id=1, source_target_pairs={{0,8},{4,12},{8,0},{12,4},{16,24},{20,28},{24,16},{28,20},{1,9},{5... | collective-permute-start | bytes 393224 | tf_op jit(solution)/shard_map/ppermute | solution.py:148
  33.9 3.9 %collective-permute-done.4 = f32[2,16,1024]{2,1,0:T(8,128)S(1)} collective-permute-done((f32[2,16,1024]{2,1,0:T(8,128)S(1)}, f32[2,16,1024]{2,1,0:T(8,128)S(1)}, u32[]{:S(2)}, u32[]{:S(2)}) %collective-permute-start.4) | collective-permute-done | bytes 131104 | tf_op jit(solution)/shard_map/ppermute | solution.py:148
  37.8 2.8 %collective-permute-start.5 = (f32[2,16,1024]{2,1,0:T(8,128)S(1)}, f32[2,16,1024]{2,1,0:T(8,128)S(1)}, u32[]{:S(2)}, u32[]{:S(2)}) collective-permute-start(f32[2,16,1024]{2,1,0:T(8,128)S(1)} %pad_maximum_fusion.1), channel_id=1, source_target_pairs={{0,16},{4,20},{8,24},{12,28},{16,0},{20,4},{24,8},{28,12},{1,17},{... | collective-permute-start | bytes 393224 | tf_op jit(solution)/shard_map/ppermute | solution.py:148
  40.7 6.1 %collective-permute-done.5 = f32[2,16,1024]{2,1,0:T(8,128)S(1)} collective-permute-done((f32[2,16,1024]{2,1,0:T(8,128)S(1)}, f32[2,16,1024]{2,1,0:T(8,128)S(1)}, u32[]{:S(2)}, u32[]{:S(2)}) %collective-permute-start.5) | collective-permute-done | bytes 131104 | tf_op jit(solution)/shard_map/ppermute | solution.py:148
  46.8 0.7 %pad_maximum_fusion.2 = f32[2,16,1024]{2,1,0:T(8,128)} fusion(f32[1,16,1024]{2,1,0:T(8,128)S(1)} %get-tuple-element.5, f32[1,16,1024]{2,1,0:T(8,128)S(1)} %get-tuple-element.4), kind=kLoop, calls=%fused_computation.2 | loop fusion | flops 32768 | bytes 262144 | tf_op jit(solution)/shard_map/stack | solution.py:153
  47.5 0.6 %fusion.1 = f32[1,16,1024]{2,1,0:T(8,128)} fusion(f32[2,16,1024]{2,1,0:T(8,128)S(1)} %collective-permute-done.5, f32[2,16,1024]{2,1,0:T(8,128)S(1)} %collective-permute-done.4, f32[2,16,1024]{2,1,0:T(8,128)S(1)} %collective-permute-done.3, pred[]{:T(512)S(6)} %ne.11, pred[]{:T(512)S(6)} %ne.10, pred[]{:T(512)S(6)} %ne.9), kind=kLoop, calls=%fused_computation.7 | loop fusion | flops 81920 | bytes 262147 | tf_op jit(solution)/shard_map/mul | solution.py:152
  (13 shorter events, 0.1 us)
Async XLA Ops:
  1.4 11.2 %collective-permute-start.2 = (f32[1,1,1024]{2,1,0:T(1,128)S(1)}, f32[1,1,1024]{2,1,0:T(1,128)S(1)}, u32[]{:S(2)}, u32[]{:S(2)}) collective-permute-start(f32[1,1,1024]{2,1,0:T(1,128)S(1)} %slice.95), channel_id=1, source_target_pairs={{5,0},{6,1},{7,2},{9,4},{10,5},{11,6},{13,8},{14,9},{15,10},{17,12... | collective-permute-start | bytes 12296 | tf_op jit(solution)/shard_map/ppermute | solution.py:26
  3.5 3.8 %copy-start.6 = (f32[8]{0:T(128)S(1)}, f32[8]{0:T(128)}, u32[]{:S(2)}) copy-start(f32[8]{0:T(128)} %param.9) | copy-start | bytes 100
  3.5 9.1 %collective-permute-start = (f32[1,16,1024]{2,1,0:T(8,128)S(1)}, f32[1,16,1024]{2,1,0:T(8,128)S(1)}, u32[]{:S(2)}, u32[]{:S(2)}) collective-permute-start(f32[1,16,1024]{2,1,0:T(8,128)S(1)} %slice.93), channel_id=1, source_target_pairs={{4,0},{8,4},{12,8},{16,12},{20,16},{24,20},{28,24},{5,1},{9,5},{13... | collective-permute-start | bytes 196616 | tf_op jit(solution)/shard_map/ppermute | solution.py:16
  6.0 1.3 %copy-start.7 = (s32[1,1,8]{2,1,0:T(1,128)S(1)}, s32[1,1,8]{2,1,0:T(1,128)}, u32[]{:S(2)}) copy-start(s32[1,1,8]{2,1,0:T(1,128)} %param.11) | copy-start | bytes 100
  6.0 6.6 %collective-permute-start.1 = (f32[16,1,1024]{2,1,0:T(1,128)S(1)}, f32[16,1,1024]{2,1,0:T(1,128)S(1)}, u32[]{:S(2)}, u32[]{:S(2)}) collective-permute-start(f32[16,1,1024]{2,1,0:T(1,128)S(1)} %slice.94), channel_id=1, source_target_pairs={{1,0},{2,1},{3,2},{5,4},{6,5},{7,6},{9,8},{10,9},{11,10},{13,12},{... | collective-permute-start | bytes 196616 | tf_op jit(solution)/shard_map/ppermute | solution.py:16
  7.4 0.7 %copy-start.4 = (f32[8]{0:T(128)S(1)}, f32[8]{0:T(128)}, u32[]{:S(2)}) copy-start(f32[8]{0:T(128)} %param.10) | copy-start | bytes 100
  7.4 0.7 %copy-start.5 = (s32[16]{0:T(128)S(1)}, s32[16]{0:T(128)}, u32[]{:S(2)}) copy-start(s32[16]{0:T(128)} %param.8) | copy-start | bytes 196
  9.7 0.8 %copy-start.3 = (s32[1024]{0:T(1024)S(1)}, s32[1024]{0:T(1024)}, u32[]{:S(2)}) copy-start(s32[1024]{0:T(1024)} %param.12) | copy-start | bytes 12292
  9.8 0.7 %copy-start.8 = (s32[16]{0:T(128)S(1)}, s32[16]{0:T(128)}, u32[]{:S(2)}) copy-start(s32[16]{0:T(128)} %param.13) | copy-start | bytes 196
  12.6 1.4 %copy-start.2 = (f32[1,1,1024]{2,1,0:T(1,128)}, f32[1,1,1024]{2,1,0:T(1,128)S(1)}, u32[]{:S(2)}) copy-start(f32[1,1,1024]{2,1,0:T(1,128)S(1)} %collective-permute-done.2.corner) | copy-start | bytes 12292
  12.6 2.7 %copy-start = (f32[1,16,1024]{2,1,0:T(8,128)}, f32[1,16,1024]{2,1,0:T(8,128)S(1)}, u32[]{:S(2)}) copy-start(f32[1,16,1024]{2,1,0:T(8,128)S(1)} %collective-permute-done.plane) | copy-start | bytes 196612
  12.6 2.7 %copy-start.1 = (f32[16,1,1024]{2,1,0:T(1,128)}, f32[16,1,1024]{2,1,0:T(1,128)S(1)}, u32[]{:S(2)}) copy-start(f32[16,1,1024]{2,1,0:T(1,128)S(1)} %collective-permute-done.1.row) | copy-start | bytes 196612
  21.6 7.7 %collective-permute-start.3 = (f32[2,16,1024]{2,1,0:T(8,128)}, f32[2,16,1024]{2,1,0:T(8,128)S(1)}, u32[]{:S(2)}, u32[]{:S(2)}) collective-permute-start(f32[2,16,1024]{2,1,0:T(8,128)} %render.1), channel_id=1, source_target_pairs={{0,4},{4,0},{8,12},{12,8},{16,20},{20,16},{24,28},{28,24},{1,5},{5... | collective-permute-start | bytes 393224 | tf_op jit(solution)/shard_map/ppermute | solution.py:148
  30.3 7.5 %collective-permute-start.4 = (f32[2,16,1024]{2,1,0:T(8,128)S(1)}, f32[2,16,1024]{2,1,0:T(8,128)S(1)}, u32[]{:S(2)}, u32[]{:S(2)}) collective-permute-start(f32[2,16,1024]{2,1,0:T(8,128)S(1)} %pad_maximum_fusion), channel_id=1, source_target_pairs={{0,8},{4,12},{8,0},{12,4},{16,24},{20,28},{24,16},{28,20},{1,9},{5... | collective-permute-start | bytes 393224 | tf_op jit(solution)/shard_map/ppermute | solution.py:148
  37.8 8.9 %collective-permute-start.5 = (f32[2,16,1024]{2,1,0:T(8,128)S(1)}, f32[2,16,1024]{2,1,0:T(8,128)S(1)}, u32[]{:S(2)}, u32[]{:S(2)}) collective-permute-start(f32[2,16,1024]{2,1,0:T(8,128)S(1)} %pad_maximum_fusion.1), channel_id=1, source_target_pairs={{0,16},{4,20},{8,24},{12,28},{16,0},{20,4},{24,8},{28,12},{1,17},{... | collective-permute-start | bytes 393224 | tf_op jit(solution)/shard_map/ppermute | solution.py:148

commit v2 on v0

v2 whole, which is shorter than its diff:
```python
import functools
import math

import jax
import jax.numpy as jnp
from jax import lax
from jax.experimental import pallas as pl
from jax.experimental.pallas import tpu as pltpu
from jax.sharding import PartitionSpec as P

SUB, LANES = 8, 128
F32 = jnp.float32
VMEM = pl.BlockSpec(memory_space=pltpu.VMEM)
SMEM = pl.BlockSpec(memory_space=pltpu.SMEM)
HBM = pl.BlockSpec(memory_space=pltpu.HBM)


def params(mib):
    return pltpu.CompilerParams(vmem_limit_bytes=mib << 20)


def from_behind(block, axis):
    size = lax.axis_size(axis)
    return lax.ppermute(block, axis, [(i + 1, i) for i in range(size - 1)])


def from_diagonal(block):
    depth, rows = lax.axis_size("depth"), lax.axis_size("rows")
    route = [
        ((z + 1) * rows + y + 1, z * rows + y)
        for z in range(depth - 1)
        for y in range(rows - 1)
    ]
    return lax.ppermute(block, ("depth", "rows"), route)


def wide(row):
    return jnp.broadcast_to(row, (SUB, LANES))


def edges_kernel(density, plane, row, corner, last_row, sems):
    height = density.shape[1]
    pieces = [
        (density.at[0, 0, :, 0, :], corner),
        (density.at[:, 0, :, 0, :], row),
        (density.at[0], plane),
        (density.at[:, height - 1, :, SUB - 1, :], last_row),
    ]
    copies = [pltpu.make_async_copy(a, b, sems.at[i]) for i, (a, b) in enumerate(pieces)]
    for copy in copies:
        copy.start()
    for copy in copies:
        copy.wait()


def hats(values, table, levels):
    def at(k):
        return wide(table[k : k + 1, :])

    absorption = [at(0) + at(1) * u for u in values]
    emission = [at(levels) + at(levels + 1) * u for u in values]
    for k in range(1, levels - 1):
        gain_a, gain_e = at(k + 1), at(levels + k + 1)
        for j, u in enumerate(values):
            kink = jnp.maximum(u, float(k))
            absorption[j] = absorption[j] + gain_a * kink
            emission[j] = emission[j] + gain_e * kink
    return absorption, emission


def interior_kernel(
    bins, absorb_bins, emit_bins, occupied, row_offsets, col_offsets, density,
    state, table, columns, rows, weights, scaled,
):
    planes, height, tiles = density.shape[:3]
    levels = bins.shape[0]
    for first, level, unit in ((0, absorb_bins, -1.0 / math.log(2.0)), (levels, emit_bins, 1.0)):
        value = [level[bins[k]] * unit for k in range(levels)]
        base, before = value[0], 0.0
        for k in range(levels - 1):
            slope = value[k + 1] - value[k]
            gain = slope - before
            before = slope
            base = base - gain * float(k)
            table[first + k + 1 : first + k + 2, :] = jnp.full((1, LANES), gain, F32)
        table[first : first + 1, :] = jnp.full((1, LANES), base, F32)

    sub = lax.broadcasted_iota(jnp.int32, (SUB, LANES), 0)
    lane_end = lax.broadcasted_iota(jnp.int32, (SUB, LANES), 1) == LANES - 1
    row_end = sub == SUB - 1
    scale = 0.5 * (levels - 1)
    near, far = [], []
    for r in range(height):
        offset = jnp.zeros((SUB, LANES), F32)
        for i in range(SUB):
            step = row_offsets[r * SUB + i].astype(F32) * (scale / 8.0)
            offset = jnp.where(sub == i, step, offset)
        far.append(offset)
        near.append(scale - offset)
        weights[0, r] = near[r]
        weights[1, r] = far[r]
    rows[0:1, :] = near[-1][SUB - 1 :, :]
    rows[1:2, :] = far[-1][SUB - 1 :, :]

    shape = (tiles, LANES)
    fraction = col_offsets[...].astype(F32) * 0.125
    ends = (lax.broadcasted_iota(jnp.int32, shape, 0) == tiles - 1) & (
        lax.broadcasted_iota(jnp.int32, shape, 1) == LANES - 1
    )
    columns[0] = 1.0 - fraction
    columns[1] = jnp.where(ends, 0.0, fraction)
    for t in range(tiles):
        columns[2, t : t + 1, :] = jnp.full((1, LANES), occupied[t].astype(F32), F32)

    for z in range(planes - 1):

        def mixed(t):
            mid = [density[z, r, t] + density[z + 1, r, t] for r in range(height)]
            up = [pltpu.roll(m, SUB - 1, 0) for m in mid]
            below = [
                jnp.where(row_end, up[r + 1], up[r]) if r + 1 < height else up[r]
                for r in range(height)
            ]
            return [near[r] * mid[r] + far[r] * below[r] for r in range(height)]

        now = mixed(0)
        turned = [pltpu.roll(m, LANES - 1, 1) for m in now]
        for t in range(tiles):
            if t + 1 < tiles:
                after = mixed(t + 1)
                after_turned = [pltpu.roll(m, LANES - 1, 1) for m in after]
            else:
                after, after_turned = now, turned
            left, right = columns[0, t : t + 1, :], columns[1, t : t + 1, :]
            for r in range(height):
                beside = jnp.where(lane_end, after_turned[r], turned[r])
                scaled[z, r, t] = left * now[r] + right * beside
            now, turned = after, after_turned

    @pl.loop(0, tiles)
    def _(t):
        mask = wide(columns[2, pl.ds(t, 1), :])
        total = [jnp.zeros((SUB, LANES), F32)] * height
        through = [jnp.ones((SUB, LANES), F32)] * height
        light = [jnp.zeros((SUB, LANES), F32)] * height
        for z in range(planes - 1):
            absorption, emission = hats([scaled[z, r, t] for r in range(height)], table, levels)
            for r in range(height):
                total[r] = total[r] + absorption[r] * mask
                behind = jnp.exp2(total[r])
                light[r] = light[r] + (through[r] - behind) * emission[r]
                through[r] = behind
        for r in range(height):
            state[0, r, t] = light[r]
            state[1, r, t] = through[r]


def boundary_kernel(
    density, plane, row, corner, last_row, table, columns, rows, weights, before, state, *, levels
):
    planes, height, tiles = density.shape[:3]
    lane_end = lax.broadcasted_iota(jnp.int32, (SUB, LANES), 1) == LANES - 1
    row_end = lax.broadcasted_iota(jnp.int32, (SUB, LANES), 0) == SUB - 1

    mid = [[density[planes - 1, r, t] + plane[r, t] for t in range(tiles)] for r in range(height)]
    up = [[pltpu.roll(m, SUB - 1, 0) for m in line] for line in mid]
    value = []
    for r in range(height):
        line = []
        for t in range(tiles):
            below = jnp.where(row_end, up[r + 1][t], up[r][t]) if r + 1 < height else up[r][t]
            line.append(weights[0, r] * mid[r][t] + weights[1, r] * below)
        turned = [pltpu.roll(m, LANES - 1, 1) for m in line]
        for t in range(tiles):
            beside = jnp.where(lane_end, turned[min(t + 1, tiles - 1)], turned[t])
            value.append(columns[0, t : t + 1, :] * line[t] + columns[1, t : t + 1, :] * beside)
    group = 4
    for first in range(0, height * tiles, group):
        where = [divmod(j, tiles) for j in range(first, min(first + group, height * tiles))]
        absorption, emission = hats(value[first : first + group], table, levels)
        for (r, t), a, e in zip(where, absorption, emission, strict=True):
            through = before[1, r, t]
            behind = through * jnp.exp2(a * wide(columns[2, t : t + 1, :]))
            state[0, r, t] = before[0, r, t] + (through - behind) * e
            state[1, r, t] = behind

    shape = (tiles, LANES)
    fold_end = lax.broadcasted_iota(jnp.int32, shape, 1) == LANES - 1
    near, far = rows[0:1, :], rows[1:2, :]
    left, right = columns[0], columns[1]
    last_plane = jnp.concatenate([plane[height - 1, t, SUB - 1 :, :] for t in range(tiles)], 0)
    own = [last_row[z] for z in range(planes)] + [last_plane]
    under = [row[z] for z in range(planes)] + [corner[...]]
    value = []
    for z in range(planes):
        line = near * (own[z] + own[z + 1]) + far * (under[z] + under[z + 1])
        turned = pltpu.roll(line, LANES - 1, 1)
        beside = jnp.where(fold_end, pltpu.roll(turned, tiles - 1, 0), turned)
        value.append(left * line + right * beside)
    total = jnp.zeros(shape, F32)
    through = jnp.ones(shape, F32)
    light = jnp.zeros(shape, F32)
    for first in range(0, planes, group):
        absorption, emission = hats(value[first : first + group], table, levels)
        for a, e in zip(absorption, emission, strict=True):
            total = total + a * columns[2]
            behind = jnp.exp2(total)
            light = light + (through - behind) * e
            through = behind
    for t in range(tiles):
        state[0, height - 1, t, SUB - 1 :, :] = light[t : t + 1, :]
        state[1, height - 1, t, SUB - 1 :, :] = through[t : t + 1, :]


def merge(state, other, front, step):
    behind = (lax.axis_index("depth") & step) != 0
    first = jnp.where(behind, other, state)
    second = jnp.where(behind, state, other)
    front = front * jnp.where(behind, other[1:], 1.0)
    return jnp.stack([first[0] + first[1] * second[0], first[1] * second[1]]), front


def on_device(density, bin_of_level, absorb_bins, emit_bins, occupancy, col_offsets, row_offsets):
    planes, rows, cols = density.shape
    height, tiles = rows // SUB, cols // LANES
    levels = bin_of_level.shape[0]
    tiled = density.reshape(planes, height, SUB, tiles, LANES).transpose(0, 1, 3, 2, 4)
    flat = (height, tiles, SUB, LANES)

    def out(*shape):
        return jax.ShapeDtypeStruct(shape, F32)

    plane, row, corner, last_row = pl.pallas_call(
        edges_kernel,
        out_shape=[
            out(*flat), out(planes, tiles, LANES), out(tiles, LANES), out(planes, tiles, LANES)
        ],
        in_specs=[HBM],
        out_specs=[VMEM] * 4,
        scratch_shapes=[pltpu.SemaphoreType.DMA((4,))],
        compiler_params=params(2),
        name="edges",
    )(tiled)
    row = from_behind(row, "rows")
    plane = from_behind(plane, "depth")
    corner = from_diagonal(corner)

    work = density.size
    state, table, columns, last_weights, row_weights = pl.pallas_call(
        interior_kernel,
        out_shape=[
            out(2, *flat), out(2 * levels, LANES), out(3, tiles, LANES), out(2, LANES),
            out(2, height, SUB, LANES),
        ],
        in_specs=[SMEM] * 5 + [VMEM] * 2,
        out_specs=[VMEM] * 5,
        scratch_shapes=[pltpu.VMEM((planes - 1, *flat), F32)],
        cost_estimate=pl.CostEstimate(
            flops=100 * work, bytes_accessed=4 * work, transcendentals=work
        ),
        compiler_params=params(8),
        name="interior",
    )(
        bin_of_level, absorb_bins, emit_bins, occupancy.reshape(tiles), row_offsets,
        col_offsets.reshape(tiles, LANES), tiled,
    )
    state = pl.pallas_call(
        functools.partial(boundary_kernel, levels=levels),
        out_shape=out(2, *flat),
        in_specs=[VMEM] * 10,
        out_specs=VMEM,
        compiler_params=params(8),
        name="boundary",
    )(tiled, plane, row, corner, last_row, table, columns, last_weights, row_weights, state)

    size = lax.axis_size("depth")
    front = jnp.ones((1, *flat), F32)
    step = 1
    while step < size:
        flip = step | (step >> 1) if 2 * step == size else step
        other = lax.ppermute(state, "depth", [(i, i ^ flip) for i in range(size)])
        state, front = merge(state, other, front, step)
        step *= 2

    def plain(block):
        return block.transpose(0, 1, 3, 2, 4).reshape(-1, rows, cols)

    return (plain(front), plain(state))


def solution(mesh):
    placed = (P("depth", "rows", None), P(), P(), P(), P("depth", "rows", None), P(), P("rows"))
    return jax.shard_map(
        on_device,
        mesh=mesh,
        in_specs=placed,
        out_specs=(P("depth", "rows", None), P(None, "rows", None)),
        check_vma=False,
    )
```

time: 161 us -> 35.1 us (0.22)
  waiting for transfers between devices: 74.8 us -> 13.7 us
  blocking collectives: 32.2 us -> 0 us
  other arithmetic: 33.3 us -> 1.45 us
  between operations: 14.2 us -> 0.81 us
  starting transfers between devices: 2.75 us -> 12.8 us
  Pallas kernels: 0 us -> 4.34 us
  local copies, waits for them, and re-layouts: 3.52 us -> 1.86 us
    psum x1 -> x0, waiting for transfers between devices: 69.7 us -> none  [on_device(): radiance = lax.psum(front * light, 'depth')]
    all_gather x1 -> x0, blocking collectives: 32.2 us -> none  [on_device(): pieces = lax.all_gather(depth_sum[None], 'depth', axis=0, tiled=True)]
    another operation x3 -> x2, other arithmetic: 31 us -> 0.02 us  [merge(): jnp.stack([first[0] + first[1] * second[0], first[1] * second[1]])]
    ppermute x2 -> x6, starting transfers between devices: 2.72 us -> 12.8 us  [the longest x3 8.75 us: on_device(): other = lax.ppermute(state, 'depth', [(i, i ^ flip) for i in range(size)])]
    ppermute x2 -> x6, waiting for transfers between devices: 5.18 us -> 13.7 us  [the longest x3 11.8 us: on_device(): other = lax.ppermute(state, 'depth', [(i, i ^ flip) for i in range(size)])]
    pallas_call x0 -> x3, Pallas kernels: none -> 4.34 us  [the longest x1 3.68 us: on_device(): pl.pallas_call(interior_kernel, out_shape=[out(2, *flat), out(2 * levels,...]
    slice x7 -> x0, local copies, waits for them, and re-layouts: 2.78 us -> none  [the longest x1 0.85 us: on_device(): following = from_behind(density[:1], 'depth', -1)]
    mul x2 -> x0, other arithmetic: 1.75 us -> none  [the longest x1 1.74 us: on_device(): mid_depth = 0.5 * (extended[:-1] + extended[1:])]
  transfers between devices with their start and end apart: 3 -> 6, of which waited for: 3 -> 4; matrix products, arithmetic and copies ran while one was open for 1% -> 0% of each run, Pallas kernels for 0% -> 11%
where the time goes in v2:
time: 35.1 us; the launch traced here: 34.9 us
  waiting for transfers between devices  13.7 us (39%)
  starting transfers between devices  12.8 us (36%)
  Pallas kernels  4.34 us (12%)
  local copies, waits for them, and re-layouts  1.86 us (5%)
  other arithmetic  1.45 us (4%)
  between operations  0.81 us (2%)
    ppermute x3, waiting for transfers between devices, on_device(): other = lax.ppermute(state, 'depth', [(i, i ^ flip) for i in range(size)])  11.8 us
    ppermute x3, starting transfers between devices, on_device(): other = lax.ppermute(state, 'depth', [(i, i ^ flip) for i in range(size)])  8.75 us
    pallas_call x1, Pallas kernels, on_device(): pl.pallas_call(interior_kernel, out_shape=[out(2, *flat), out(2 * levels,...  3.68 us
    ppermute x2, starting transfers between devices, from_behind(): return lax.ppermute(block, axis, [(i + 1, i) for i in range(size - 1)])  2.72 us
    unnamed x16, local copies, waits for them, and re-layouts  1.86 us
    ppermute x1, waiting for transfers between devices, from_diagonal(): return lax.ppermute(block, ('depth', 'rows'), route)  1.84 us
    reshape x2, other arithmetic, plain(): return block.transpose(0, 1, 3, 2, 4).reshape(-1, rows, cols)  1.31 us
    ppermute x1, starting transfers between devices, from_diagonal(): return lax.ppermute(block, ('depth', 'rows'), route)  1.29 us
  transfers between devices with their start and end apart: 6, of which 4 were waited for; matrix products, arithmetic and copies ran while one was open for 0% of the time, Pallas kernels for 11%

profile of v2, /device:TPU:0, one launch (start us, length us, event | category | flops | bytes accessed | tf_op | source)
XLA Modules:
  0.0 34.9 jit_solution(1840874852732205591)
XLA Ops:
  0.6 0.0 copy-start
  0.6 1.2 %copy-done = f32[16,16,1024]{2,1,0:T(8,128)S(1)} copy-done((f32[16,16,1024]{2,1,0:T(8,128)S(1)}, f32[16,16,1024]{2,1,0:T(8,128)}, u32[]{:S(2)}) %copy-start) | copy-done | bytes 1048600
  1.9 0.0 copy-start.1
  1.9 0.0 copy-start.6
  1.9 0.0 copy-start.7
  1.9 0.2 edges.1
  2.1 0.0 copy-start.2
  2.1 1.4 %collective-permute-start = (f32[2,8,8,128]{3,2,1,0:T(8,128)S(1)}, f32[2,8,8,128]{3,2,1,0:T(8,128)S(1)}, u32[]{:S(2)}, u32[]{:S(2)}) collective-permute-start(f32[2,8,8,128]{3,2,1,0:T(8,128)S(1)} %get-tuple-element.11), channel_id=1, source_target_pairs={{4,0},{8,4},{12,8},{16,12},{20,16},{24,20},{28,24},{5,1},{9,5},{13... | collective-permute-start | bytes 196616 | tf_op jit(solution)/shard_map/ppermute | solution.py:24
  3.5 1.3 %collective-permute-start.1 = (f32[16,8,128]{2,1,0:T(8,128)S(1)}, f32[16,8,128]{2,1,0:T(8,128)S(1)}, u32[]{:S(2)}, u32[]{:S(2)}) collective-permute-start(f32[16,8,128]{2,1,0:T(8,128)S(1)} %get-tuple-element.12), channel_id=1, source_target_pairs={{1,0},{2,1},{3,2},{5,4},{6,5},{7,6},{9,8},{10,9},{11,10},{13,12},{... | collective-permute-start | bytes 196616 | tf_op jit(solution)/shard_map/ppermute | solution.py:24
  4.8 1.3 %collective-permute-start.2 = (f32[8,128]{1,0:T(8,128)S(1)}, f32[8,128]{1,0:T(8,128)S(1)}, u32[]{:S(2)}, u32[]{:S(2)}) collective-permute-start(f32[8,128]{1,0:T(8,128)S(1)} %get-tuple-element.13), channel_id=1, source_target_pairs={{5,0},{6,1},{7,2},{9,4},{10,5},{11,6},{13,8},{14,9},{15,10},{17,12... | collective-permute-start | bytes 12296 | tf_op jit(solution)/shard_map/ppermute | solution.py:34
  6.1 0.0 copy-start.3
  6.1 0.0 copy-start.4
  6.2 0.0 copy-start.5
  6.2 0.0 copy-done.1
  6.2 0.0 copy-done.6
  6.2 0.0 copy-done.7
  6.2 0.0 copy-done.2
  6.2 0.6 %copy-done.3 = s32[16]{0:T(128)S(1)} copy-done((s32[16]{0:T(128)S(1)}, s32[16]{0:T(128)}, u32[]{:S(2)}) %copy-start.3) | copy-done | bytes 88
  6.8 0.0 copy-done.4
  6.8 0.0 copy-done.5
  6.8 3.7 %interior.1 = (f32[2,2,8,8,128]{4,3,2,1,0:T(8,128)S(1)}, f32[32,128]{1,0:T(8,128)S(1)}, f32[3,8,128]{2,1,0:T(8,128)S(1)}, f32[2,128]{1,0:T(2,128)S(1)}, f32[2,2,8,128]{3,2,1,0:T(8,128)S(1)}) custom-call(s32[16]{0:T(128)S(1)} %copy-done.3, f32[8]{0:T(128)S(1)} %copy-done.4, f32[8]{0:T(128)S(1)} %copy-done.5, s32[8]{0:T(128)S(1)} %bitcast.17, ...), custom_call_target="tpu_custom_call" | custom-call | flops 26214400 | bytes 1048576 | tf_op jit(solution)/shard_map/interior/pallas_call | solution.py:249
  10.5 1.8 %collective-permute-done.2.corner = f32[8,128]{1,0:T(8,128)S(1)} collective-permute-done((f32[8,128]{1,0:T(8,128)S(1)}, f32[8,128]{1,0:T(8,128)S(1)}, u32[]{:S(2)}, u32[]{:S(2)}) %collective-permute-start.2) | collective-permute-done | bytes 4128 | tf_op jit(solution)/shard_map/ppermute | solution.py:34
  12.3 0.0 collective-permute-done.plane
  12.4 0.0 collective-permute-done.1.row
  12.4 0.4 %boundary.1 = f32[2,2,8,8,128]{4,3,2,1,0:T(8,128)S(1)} custom-call(f32[16,2,8,8,128]{4,3,2,1,0:T(8,128)S(1)} %bitcast.15, f32[2,8,8,128]{3,2,1,0:T(8,128)S(1)} %collective-permute-done.plane, f32[16,8,128]{2,1,0:T(8,128)S(1)} %collective-permute-done.1.row, f32[8,128]{1,0:T(8,128)S(1)} %collective-permute-done.2.corner, ...), custom_call_target="tpu_custom_call" | custom-call | tf_op jit(solution)/shard_map/boundary/pallas_call | solution.py:267
  12.8 3.0 %collective-permute-start.3 = (f32[2,2,8,8,128]{4,3,2,1,0:T(8,128)S(1)}, f32[2,2,8,8,128]{4,3,2,1,0:T(8,128)S(1)}, u32[]{:S(2)}, u32[]{:S(2)}) collective-permute-start(f32[2,2,8,8,128]{4,3,2,1,0:T(8,128)S(1)} %boundary.1), channel_id=1, source_target_pairs={{0,4},{4,0},{8,12},{12,8},{16,20},{20,16},{24,28},{28,24},{1,5},{5... | collective-permute-start | bytes 393224 | tf_op jit(solution)/shard_map/ppermute | solution.py:281
  15.8 4.0 %collective-permute-done.3 = f32[2,2,8,8,128]{4,3,2,1,0:T(8,128)S(1)} collective-permute-done((f32[2,2,8,8,128]{4,3,2,1,0:T(8,128)S(1)}, f32[2,2,8,8,128]{4,3,2,1,0:T(8,128)S(1)}, u32[]{:S(2)}, u32[]{:S(2)}) %collective-permute-start.3) | collective-permute-done | bytes 131104 | tf_op jit(solution)/shard_map/ppermute | solution.py:281
  19.9 1.9 %collective-permute-start.4 = (f32[2,2,8,8,128]{4,3,2,1,0:T(8,128)S(1)}, f32[2,2,8,8,128]{4,3,2,1,0:T(8,128)S(1)}, u32[]{:S(2)}, u32[]{:S(2)}) collective-permute-start(f32[2,2,8,8,128]{4,3,2,1,0:T(8,128)S(1)} %pad_maximum_fusion), channel_id=1, source_target_pairs={{0,8},{4,12},{8,0},{12,4},{16,24},{20,28},{24,16},{28,20},{1,9},{5... | collective-permute-start | bytes 393224 | tf_op jit(solution)/shard_map/ppermute | solution.py:281
  21.8 4.3 %collective-permute-done.4 = f32[2,2,8,8,128]{4,3,2,1,0:T(8,128)S(1)} collective-permute-done((f32[2,2,8,8,128]{4,3,2,1,0:T(8,128)S(1)}, f32[2,2,8,8,128]{4,3,2,1,0:T(8,128)S(1)}, u32[]{:S(2)}, u32[]{:S(2)}) %collective-permute-start.4) | collective-permute-done | bytes 131104 | tf_op jit(solution)/shard_map/ppermute | solution.py:281
  26.2 3.8 %collective-permute-start.5 = (f32[2,2,8,8,128]{4,3,2,1,0:T(8,128)S(1)}, f32[2,2,8,8,128]{4,3,2,1,0:T(8,128)S(1)}, u32[]{:S(2)}, u32[]{:S(2)}) collective-permute-start(f32[2,2,8,8,128]{4,3,2,1,0:T(8,128)S(1)} %pad_maximum_fusion.1), channel_id=1, source_target_pairs={{0,24},{4,28},{8,16},{12,20},{16,8},{20,12},{24,0},{28,4},{1,25},{... | collective-permute-start | bytes 393224 | tf_op jit(solution)/shard_map/ppermute | solution.py:281
  30.0 3.5 %collective-permute-done.5 = f32[2,2,8,8,128]{4,3,2,1,0:T(8,128)S(1)} collective-permute-done((f32[2,2,8,8,128]{4,3,2,1,0:T(8,128)S(1)}, f32[2,2,8,8,128]{4,3,2,1,0:T(8,128)S(1)}, u32[]{:S(2)}, u32[]{:S(2)}) %collective-permute-start.5) | collective-permute-done | bytes 131104 | tf_op jit(solution)/shard_map/ppermute | solution.py:281
  33.6 0.7 %maximum_bitcast_fusion = f32[2,16,1024]{2,1,0:T(8,128)} fusion(f32[1,2,8,8,128]{4,3,2,1,0:T(8,128)S(1)} %get-tuple-element.21, f32[1,2,8,8,128]{4,3,2,1,0:T(8,128)S(1)} %get-tuple-element.20), kind=kLoop, calls=%fused_computation.2 | loop fusion | flops 32768 | bytes 262144 | tf_op jit(solution)/shard_map/reshape | solution.py:286
  34.2 0.6 %fusion.2 = f32[1,16,1024]{2,1,0:T(8,128)} fusion(f32[2,2,8,8,128]{4,3,2,1,0:T(8,128)S(1)} %collective-permute-done.5, f32[2,2,8,8,128]{4,3,2,1,0:T(8,128)S(1)} %collective-permute-done.4, f32[2,2,8,8,128]{4,3,2,1,0:T(8,128)S(1)} %collective-permute-done.3, pred[]{:T(512)S(6)} %ne.11, pred[]{:T(512)S(6)} %ne.10, pred[]{:T(512)S(6)} %ne.9), kind=kLoop, calls=%fused_computation.8 | loop fusion | flops 81920 | bytes 262147 | tf_op jit(solution)/shard_map/reshape | solution.py:286
  (8 shorter events, 0.1 us)
Async XLA Ops:
  0.6 1.2 %copy-start = (f32[16,16,1024]{2,1,0:T(8,128)S(1)}, f32[16,16,1024]{2,1,0:T(8,128)}, u32[]{:S(2)}) copy-start(f32[16,16,1024]{2,1,0:T(8,128)} %param.7) | copy-start | bytes 3145732
  1.9 4.3 %copy-start.1 = (f32[16,16,1024]{2,1,0:T(8,128)S(1)}, f32[16,16,1024]{2,1,0:T(8,128)}, u32[]{:S(2)}) copy-start(f32[16,16,1024]{2,1,0:T(8,128)} %param.7) | copy-start | bytes 3145732
  1.9 4.3 %copy-start.6 = (s32[1,1,8]{2,1,0:T(1,128)S(1)}, s32[1,1,8]{2,1,0:T(1,128)}, u32[]{:S(2)}) copy-start(s32[1,1,8]{2,1,0:T(1,128)} %param.11) | copy-start | bytes 100
  1.9 4.3 %copy-start.7 = (s32[16]{0:T(128)S(1)}, s32[16]{0:T(128)}, u32[]{:S(2)}) copy-start(s32[16]{0:T(128)} %row_offsets.1) | copy-start | bytes 196
  2.1 4.1 %copy-start.2 = (s32[1024]{0:T(1024)S(1)}, s32[1024]{0:T(1024)}, u32[]{:S(2)}) copy-start(s32[1024]{0:T(1024)} %param.12) | copy-start | bytes 12292
  2.1 10.3 %collective-permute-start = (f32[2,8,8,128]{3,2,1,0:T(8,128)S(1)}, f32[2,8,8,128]{3,2,1,0:T(8,128)S(1)}, u32[]{:S(2)}, u32[]{:S(2)}) collective-permute-start(f32[2,8,8,128]{3,2,1,0:T(8,128)S(1)} %get-tuple-element.11), channel_id=1, source_target_pairs={{4,0},{8,4},{12,8},{16,12},{20,16},{24,20},{28,24},{5,1},{9,5},{13... | collective-permute-start | bytes 196616 | tf_op jit(solution)/shard_map/ppermute | solution.py:24
  3.5 8.8 %collective-permute-start.1 = (f32[16,8,128]{2,1,0:T(8,128)S(1)}, f32[16,8,128]{2,1,0:T(8,128)S(1)}, u32[]{:S(2)}, u32[]{:S(2)}) collective-permute-start(f32[16,8,128]{2,1,0:T(8,128)S(1)} %get-tuple-element.12), channel_id=1, source_target_pairs={{1,0},{2,1},{3,2},{5,4},{6,5},{7,6},{9,8},{10,9},{11,10},{13,12},{... | collective-permute-start | bytes 196616 | tf_op jit(solution)/shard_map/ppermute | solution.py:24
  4.8 7.5 %collective-permute-start.2 = (f32[8,128]{1,0:T(8,128)S(1)}, f32[8,128]{1,0:T(8,128)S(1)}, u32[]{:S(2)}, u32[]{:S(2)}) collective-permute-start(f32[8,128]{1,0:T(8,128)S(1)} %get-tuple-element.13), channel_id=1, source_target_pairs={{5,0},{6,1},{7,2},{9,4},{10,5},{11,6},{13,8},{14,9},{15,10},{17,12... | collective-permute-start | bytes 12296 | tf_op jit(solution)/shard_map/ppermute | solution.py:34
  6.1 0.7 %copy-start.3 = (s32[16]{0:T(128)S(1)}, s32[16]{0:T(128)}, u32[]{:S(2)}) copy-start(s32[16]{0:T(128)} %bins.1) | copy-start | bytes 196
  6.1 0.7 %copy-start.4 = (f32[8]{0:T(128)S(1)}, f32[8]{0:T(128)}, u32[]{:S(2)}) copy-start(f32[8]{0:T(128)} %absorb_bins.1) | copy-start | bytes 100
  6.2 0.7 %copy-start.5 = (f32[8]{0:T(128)S(1)}, f32[8]{0:T(128)}, u32[]{:S(2)}) copy-start(f32[8]{0:T(128)} %emit_bins.1) | copy-start | bytes 100
  12.8 7.0 %collective-permute-start.3 = (f32[2,2,8,8,128]{4,3,2,1,0:T(8,128)S(1)}, f32[2,2,8,8,128]{4,3,2,1,0:T(8,128)S(1)}, u32[]{:S(2)}, u32[]{:S(2)}) collective-permute-start(f32[2,2,8,8,128]{4,3,2,1,0:T(8,128)S(1)} %boundary.1), channel_id=1, source_target_pairs={{0,4},{4,0},{8,12},{12,8},{16,20},{20,16},{24,28},{28,24},{1,5},{5... | collective-permute-start | bytes 393224 | tf_op jit(solution)/shard_map/ppermute | solution.py:281
  19.9 6.2 %collective-permute-start.4 = (f32[2,2,8,8,128]{4,3,2,1,0:T(8,128)S(1)}, f32[2,2,8,8,128]{4,3,2,1,0:T(8,128)S(1)}, u32[]{:S(2)}, u32[]{:S(2)}) collective-permute-start(f32[2,2,8,8,128]{4,3,2,1,0:T(8,128)S(1)} %pad_maximum_fusion), channel_id=1, source_target_pairs={{0,8},{4,12},{8,0},{12,4},{16,24},{20,28},{24,16},{28,20},{1,9},{5... | collective-permute-start | bytes 393224 | tf_op jit(solution)/shard_map/ppermute | solution.py:281
  26.2 7.3 %collective-permute-start.5 = (f32[2,2,8,8,128]{4,3,2,1,0:T(8,128)S(1)}, f32[2,2,8,8,128]{4,3,2,1,0:T(8,128)S(1)}, u32[]{:S(2)}, u32[]{:S(2)}) collective-permute-start(f32[2,2,8,8,128]{4,3,2,1,0:T(8,128)S(1)} %pad_maximum_fusion.1), channel_id=1, source_target_pairs={{0,24},{4,28},{8,16},{12,20},{16,8},{20,12},{24,0},{28,4},{1,25},{... | collective-permute-start | bytes 393224 | tf_op jit(solution)/shard_map/ppermute | solution.py:281

commit v3 on v2

--- a/solution.py
+++ b/solution.py
@@ -38,7 +38,10 @@
     return jnp.broadcast_to(row, (SUB, LANES))
 
 
-def edges_kernel(density, plane, row, corner, last_row, sems):
+def edges_kernel(
+    density, bins, absorb_bins, emit_bins, occupied, row_offsets, col_offsets,
+    plane, row, corner, last_row, small, columns, sems,
+):
     height = density.shape[1]
     pieces = [
         (density.at[0, 0, :, 0, :], corner),
@@ -49,6 +52,16 @@
     copies = [pltpu.make_async_copy(a, b, sems.at[i]) for i, (a, b) in enumerate(pieces)]
     for copy in copies:
         copy.start()
+    small[...] = jnp.zeros_like(small)
+    for i, source in enumerate((bins, absorb_bins, emit_bins, occupied, row_offsets)):
+        small[i : i + 1, : source.shape[1]] = source[...].astype(F32)
+    fraction = col_offsets[...].astype(F32) * 0.125
+    shape = fraction.shape
+    ends = (lax.broadcasted_iota(jnp.int32, shape, 0) == shape[0] - 1) & (
+        lax.broadcasted_iota(jnp.int32, shape, 1) == LANES - 1
+    )
+    columns[0] = 1.0 - fraction
+    columns[1] = jnp.where(ends, 0.0, fraction)
     for copy in copies:
         copy.wait()
 
@@ -68,49 +81,43 @@
     return absorption, emission
 
 
-def interior_kernel(
-    bins, absorb_bins, emit_bins, occupied, row_offsets, col_offsets, density,
-    state, table, columns, rows, weights, scaled,
-):
+def interior_kernel(small, columns, density, state, table, masks, rows, weights, scaled, *, levels):
     planes, height, tiles = density.shape[:3]
-    levels = bins.shape[0]
-    for first, level, unit in ((0, absorb_bins, -1.0 / math.log(2.0)), (levels, emit_bins, 1.0)):
-        value = [level[bins[k]] * unit for k in range(levels)]
-        base, before = value[0], 0.0
-        for k in range(levels - 1):
-            slope = value[k + 1] - value[k]
-            gain = slope - before
-            before = slope
-            base = base - gain * float(k)
-            table[first + k + 1 : first + k + 2, :] = jnp.full((1, LANES), gain, F32)
-        table[first : first + 1, :] = jnp.full((1, LANES), base, F32)
-
+    lane = lax.broadcasted_iota(jnp.int32, (SUB, LANES), 1)
     sub = lax.broadcasted_iota(jnp.int32, (SUB, LANES), 0)
-    lane_end = lax.broadcasted_iota(jnp.int32, (SUB, LANES), 1) == LANES - 1
-    row_end = sub == SUB - 1
+    lane_end, row_end = lane == LANES - 1, sub == SUB - 1
+    bins, absorb_bins, emit_bins, occupied, row_offsets = (
+        wide(small[i : i + 1, :]) for i in range(5)
+    )
+
+    def pick(vector, k):
+        return jnp.broadcast_to(vector[:, k : k + 1], (SUB, LANES))
+
     scale = 0.5 * (levels - 1)
     near, far = [], []
     for r in range(height):
         offset = jnp.zeros((SUB, LANES), F32)
         for i in range(SUB):
-            step = row_offsets[r * SUB + i].astype(F32) * (scale / 8.0)
-            offset = jnp.where(sub == i, step, offset)
-        far.append(offset)
-        near.append(scale - offset)
+            offset = jnp.where(sub == i, pick(row_offsets, r * SUB + i), offset)
+        far.append(offset * (scale / 8.0))
+        near.append(scale - far[r])
         weights[0, r] = near[r]
         weights[1, r] = far[r]
     rows[0:1, :] = near[-1][SUB - 1 :, :]
     rows[1:2, :] = far[-1][SUB - 1 :, :]
-
-    shape = (tiles, LANES)
-    fraction = col_offsets[...].astype(F32) * 0.125
-    ends = (lax.broadcasted_iota(jnp.int32, shape, 0) == tiles - 1) & (
-        lax.broadcasted_iota(jnp.int32, shape, 1) == LANES - 1
-    )
-    columns[0] = 1.0 - fraction
-    columns[1] = jnp.where(ends, 0.0, fraction)
     for t in range(tiles):
-        columns[2, t : t + 1, :] = jnp.full((1, LANES), occupied[t].astype(F32), F32)
+        masks[t : t + 1, :] = pick(occupied, t)[:1, :]
+
+    which = bins.astype(jnp.int32)
+    for first, level, unit in ((0, absorb_bins, -1.0 / math.log(2.0)), (levels, emit_bins, 1.0)):
+        value = jnp.take_along_axis(level, which, axis=1, mode="promise_in_bounds") * unit
+        slope = pltpu.roll(value, LANES - 1, 1) - value
+        gain = jnp.where(lane == 0, slope, slope - pltpu.roll(slope, 1, 1))
+        shift = jnp.where(lane < levels - 1, gain * lane.astype(F32), 0.0)
+        base = pick(value, 0) - jnp.sum(shift, 1, keepdims=True)
+        table[first : first + 1, :] = base[:1, :]
+        for k in range(levels - 1):
+            table[first + k + 1 : first + k + 2, :] = pick(gain, k)[:1, :]
 
     for z in range(planes - 1):
 
@@ -139,7 +146,7 @@
 
     @pl.loop(0, tiles)
     def _(t):
-        mask = wide(columns[2, pl.ds(t, 1), :])
+        mask = wide(masks[pl.ds(t, 1), :])
         total = [jnp.zeros((SUB, LANES), F32)] * height
         through = [jnp.ones((SUB, LANES), F32)] * height
         light = [jnp.zeros((SUB, LANES), F32)] * height
@@ -156,7 +163,7 @@
 
 
 def boundary_kernel(
-    density, plane, row, corner, last_row, table, columns, rows, weights, before, state, *, levels
+    density, plane, row, corner, last_row, table, columns, masks, rows, weights, before, state, *, levels
 ):
     planes, height, tiles = density.shape[:3]
     lane_end = lax.broadcasted_iota(jnp.int32, (SUB, LANES), 1) == LANES - 1
@@ -180,7 +187,7 @@
         absorption, emission = hats(value[first : first + group], table, levels)
         for (r, t), a, e in zip(where, absorption, emission, strict=True):
             through = before[1, r, t]
-            behind = through * jnp.exp2(a * wide(columns[2, t : t + 1, :]))
+            behind = through * jnp.exp2(a * wide(masks[t : t + 1, :]))
             state[0, r, t] = before[0, r, t] + (through - behind) * e
             state[1, r, t] = behind
 
@@ -203,7 +210,7 @@
     for first in range(0, planes, group):
         absorption, emission = hats(value[first : first + group], table, levels)
         for a, e in zip(absorption, emission, strict=True):
-            total = total + a * columns[2]
+            total = total + a * masks[...]
             behind = jnp.exp2(total)
             light = light + (through - behind) * e
             through = behind
@@ -212,12 +219,33 @@
         state[1, height - 1, t, SUB - 1 :, :] = through[t : t + 1, :]
 
 
+def is_behind(step):
+    return (lax.axis_index("depth") & step) != 0
+
+
 def merge(state, other, front, step):
-    behind = (lax.axis_index("depth") & step) != 0
+    behind = is_behind(step)
     first = jnp.where(behind, other, state)
     second = jnp.where(behind, state, other)
     front = front * jnp.where(behind, other[1:], 1.0)
     return jnp.stack([first[0] + first[1] * second[0], first[1] * second[1]]), front
+
+
+def last_merge_kernel(state, other, front, front_out, image_out, front_buf, image_buf, sems, *, step):
+    behind = is_behind(step)
+    light, through = state[0], state[1]
+    other_light, other_through = other[0], other[1]
+    front_buf[0] = front[0] * jnp.where(behind, other_through, 1.0)
+    copy_front = pltpu.make_async_copy(front_buf, front_out, sems.at[0])
+    copy_front.start()
+    image_buf[0] = jnp.where(
+        behind, other_light + other_through * light, light + through * other_light
+    )
+    image_buf[1] = through * other_through
+    copy_image = pltpu.make_async_copy(image_buf, image_out, sems.at[1])
+    copy_image.start()
+    copy_front.wait()
+    copy_image.wait()
 
 
 def on_device(density, bin_of_level, absorb_bins, emit_bins, occupancy, col_offsets, row_offsets):
@@ -230,29 +258,33 @@
     def out(*shape):
         return jax.ShapeDtypeStruct(shape, F32)
 
-    plane, row, corner, last_row = pl.pallas_call(
+    plane, row, corner, last_row, small, columns = pl.pallas_call(
         edges_kernel,
         out_shape=[
-            out(*flat), out(planes, tiles, LANES), out(tiles, LANES), out(planes, tiles, LANES)
+            out(*flat), out(planes, tiles, LANES), out(tiles, LANES), out(planes, tiles, LANES),
+            out(SUB, LANES), out(2, tiles, LANES),
         ],
-        in_specs=[HBM],
-        out_specs=[VMEM] * 4,
+        in_specs=[HBM] + [VMEM] * 6,
+        out_specs=[VMEM] * 6,
         scratch_shapes=[pltpu.SemaphoreType.DMA((4,))],
         compiler_params=params(2),
         name="edges",
-    )(tiled)
+    )(
+        tiled, bin_of_level[None], absorb_bins[None], emit_bins[None],
+        occupancy.reshape(1, tiles), row_offsets[None], col_offsets.reshape(tiles, LANES),
+    )
     row = from_behind(row, "rows")
     plane = from_behind(plane, "depth")
     corner = from_diagonal(corner)
 
     work = density.size
-    state, table, columns, last_weights, row_weights = pl.pallas_call(
-        interior_kernel,
+    state, table, masks, last_weights, row_weights = pl.pallas_call(
+        functools.partial(interior_kernel, levels=levels),
         out_shape=[
-            out(2, *flat), out(2 * levels, LANES), out(3, tiles, LANES), out(2, LANES),
+            out(2, *flat), out(2 * levels, LANES), out(tiles, LANES), out(2, LANES),
             out(2, height, SUB, LANES),
         ],
-        in_specs=[SMEM] * 5 + [VMEM] * 2,
+        in_specs=[VMEM] * 3,
         out_specs=[VMEM] * 5,
         scratch_shapes=[pltpu.VMEM((planes - 1, *flat), F32)],
         cost_estimate=pl.CostEstimate(
@@ -260,27 +292,36 @@
         ),
         compiler_params=params(8),
         name="interior",
-    )(
-        bin_of_level, absorb_bins, emit_bins, occupancy.reshape(tiles), row_offsets,
-        col_offsets.reshape(tiles, LANES), tiled,
-    )
+    )(small, columns, tiled)
     state = pl.pallas_call(
         functools.partial(boundary_kernel, levels=levels),
         out_shape=out(2, *flat),
-        in_specs=[VMEM] * 10,
+        in_specs=[VMEM] * 11,
         out_specs=VMEM,
         compiler_params=params(8),
         name="boundary",
-    )(tiled, plane, row, corner, last_row, table, columns, last_weights, row_weights, state)
+    )(tiled, plane, row, corner, last_row, table, columns, masks, last_weights, row_weights, state)
 
     size = lax.axis_size("depth")
     front = jnp.ones((1, *flat), F32)
     step = 1
-    while step < size:
-        flip = step | (step >> 1) if 2 * step == size else step
-        other = lax.ppermute(state, "depth", [(i, i ^ flip) for i in range(size)])
+    while 2 * step < size:
+        other = lax.ppermute(state, "depth", [(i, i ^ step) for i in range(size)])
         state, front = merge(state, other, front, step)
         step *= 2
+    flip = step | (step >> 1)
+    other = lax.ppermute(state, "depth", [(i, i ^ flip) for i in range(size)])
+    front, state = pl.pallas_call(
+        functools.partial(last_merge_kernel, step=step),
+        out_shape=[out(1, *flat), out(2, *flat)],
+        in_specs=[VMEM] * 3,
+        out_specs=[HBM] * 2,
+        scratch_shapes=[
+            pltpu.VMEM((1, *flat), F32), pltpu.VMEM((2, *flat), F32), pltpu.SemaphoreType.DMA((2,))
+        ],
+        compiler_params=params(4),
+        name="last_merge",
+    )(state, other, front)
 
     def plain(block):
         return block.transpose(0, 1, 3, 2, 4).reshape(-1, rows, cols)

time: 35.1 us -> 34.7 us (0.989)
  waiting for transfers between devices: 13.7 us -> 15.3 us
  other arithmetic: 1.45 us -> 0.11 us
  starting transfers between devices: 12.8 us -> 11.6 us
  Pallas kernels: 4.34 us -> 4.76 us
    ppermute x0 -> x2, waiting for transfers between devices: none -> 8.7 us  [on_device(): other = lax.ppermute(state, 'depth', [(i, i ^ step) for i in range(size)])]
    ppermute x3 -> x1, waiting for transfers between devices: 11.8 us -> 3.77 us  [on_device(): other = lax.ppermute(state, 'depth', [(i, i ^ flip) for i in range(size)])]
    ppermute x3 -> x1, starting transfers between devices: 8.75 us -> 3.65 us  [on_device(): other = lax.ppermute(state, 'depth', [(i, i ^ flip) for i in range(size)])]
    ppermute x0 -> x2, starting transfers between devices: none -> 3.92 us  [on_device(): other = lax.ppermute(state, 'depth', [(i, i ^ step) for i in range(size)])]
    reshape x2 -> x0, other arithmetic: 1.31 us -> none  [plain(): return block.transpose(0, 1, 3, 2, 4).reshape(-1, rows, cols)]
    ppermute x1, waiting for transfers between devices: 1.84 us -> 2.82 us  [from_diagonal(): return lax.ppermute(block, ('depth', 'rows'), route)]
    pallas_call x1 -> x2, Pallas kernels: 3.68 us -> 4.1 us  [the longest x1 3.39 us: on_device(): pl.pallas_call(functools.partial(interior_kernel, levels=levels), out_sha...]
  transfers between devices with their start and end apart: 6 -> 6, of which waited for: 4 -> 4; matrix products, arithmetic and copies ran while one was open for 0% -> 0% of each run, Pallas kernels for 11% -> 10%
where the time goes in v3:
time: 34.7 us; the launch traced here: 34.4 us
  waiting for transfers between devices  15.3 us (44%)
  starting transfers between devices  11.6 us (33%)
  Pallas kernels  4.76 us (14%)
  local copies, waits for them, and re-layouts  1.91 us (6%)
  between operations  0.79 us (2%)
    ppermute x2, waiting for transfers between devices, on_device(): other = lax.ppermute(state, 'depth', [(i, i ^ step) for i in range(size)])  8.7 us
    ppermute x2, starting transfers between devices, on_device(): other = lax.ppermute(state, 'depth', [(i, i ^ step) for i in range(size)])  3.92 us
    ppermute x1, waiting for transfers between devices, on_device(): other = lax.ppermute(state, 'depth', [(i, i ^ flip) for i in range(size)])  3.77 us
    ppermute x1, starting transfers between devices, on_device(): other = lax.ppermute(state, 'depth', [(i, i ^ flip) for i in range(size)])  3.65 us
    pallas_call x1, Pallas kernels, on_device(): pl.pallas_call(functools.partial(interior_kernel, levels=levels), out_sha...  3.39 us
    ppermute x1, waiting for transfers between devices, from_diagonal(): return lax.ppermute(block, ('depth', 'rows'), route)  2.82 us
    ppermute x2, starting transfers between devices, from_behind(): return lax.ppermute(block, axis, [(i + 1, i) for i in range(size - 1)])  2.72 us
    unnamed x16, local copies, waits for them, and re-layouts  1.91 us
  transfers between devices with their start and end apart: 6, of which 4 were waited for; matrix products, arithmetic and copies ran while one was open for 0% of the time, Pallas kernels for 10%

profile of v3, /device:TPU:0, one launch (start us, length us, event | category | flops | bytes accessed | tf_op | source)
XLA Modules:
  0.0 34.4 jit_solution(18245180485485126280)
XLA Ops:
  0.6 0.0 copy-start.2
  0.6 0.0 copy-start.6
  0.7 0.0 copy-start.7
  0.7 0.0 copy-start.3
  0.7 0.0 copy-start.4
  0.7 0.0 copy-start.5
  0.7 0.6 %copy-done.2 = s32[1024]{0:T(1024)S(1)} copy-done((s32[1024]{0:T(1024)S(1)}, s32[1024]{0:T(1024)}, u32[]{:S(2)}) %copy-start.2) | copy-done | bytes 4120
  1.3 0.0 copy-done.6
  1.3 0.0 copy-done.7
  1.3 0.0 copy-done.3
  1.3 0.0 copy-done.4
  1.4 0.0 copy-done.5
  1.4 0.0 copy-start
  1.4 1.2 %copy-done = f32[16,16,1024]{2,1,0:T(8,128)S(1)} copy-done((f32[16,16,1024]{2,1,0:T(8,128)S(1)}, f32[16,16,1024]{2,1,0:T(8,128)}, u32[]{:S(2)}) %copy-start) | copy-done | bytes 1048600
  2.6 0.0 copy-start.1
  2.6 0.2 edges.1
  2.8 1.4 %collective-permute-start = (f32[2,8,8,128]{3,2,1,0:T(8,128)S(1)}, f32[2,8,8,128]{3,2,1,0:T(8,128)S(1)}, u32[]{:S(2)}, u32[]{:S(2)}) collective-permute-start(f32[2,8,8,128]{3,2,1,0:T(8,128)S(1)} %get-tuple-element.15), channel_id=1, source_target_pairs={{4,0},{8,4},{12,8},{16,12},{20,16},{24,20},{28,24},{5,1},{9,5},{13... | collective-permute-start | bytes 196616 | tf_op jit(solution)/shard_map/ppermute | solution.py:24
  4.3 1.3 %collective-permute-start.1 = (f32[16,8,128]{2,1,0:T(8,128)S(1)}, f32[16,8,128]{2,1,0:T(8,128)S(1)}, u32[]{:S(2)}, u32[]{:S(2)}) collective-permute-start(f32[16,8,128]{2,1,0:T(8,128)S(1)} %get-tuple-element.16), channel_id=1, source_target_pairs={{1,0},{2,1},{3,2},{5,4},{6,5},{7,6},{9,8},{10,9},{11,10},{13,12},{... | collective-permute-start | bytes 196616 | tf_op jit(solution)/shard_map/ppermute | solution.py:24
  5.6 1.3 %collective-permute-start.2 = (f32[8,128]{1,0:T(8,128)S(1)}, f32[8,128]{1,0:T(8,128)S(1)}, u32[]{:S(2)}, u32[]{:S(2)}) collective-permute-start(f32[8,128]{1,0:T(8,128)S(1)} %get-tuple-element.17), channel_id=1, source_target_pairs={{5,0},{6,1},{7,2},{9,4},{10,5},{11,6},{13,8},{14,9},{15,10},{17,12... | collective-permute-start | bytes 12296 | tf_op jit(solution)/shard_map/ppermute | solution.py:34
  6.9 0.0 copy-done.1
  6.9 3.4 %interior.1 = (f32[2,2,8,8,128]{4,3,2,1,0:T(8,128)S(1)}, f32[32,128]{1,0:T(8,128)S(1)}, f32[8,128]{1,0:T(8,128)S(1)}, f32[2,128]{1,0:T(2,128)S(1)}, f32[2,2,8,128]{3,2,1,0:T(8,128)S(1)}) custom-call(f32[8,128]{1,0:T(8,128)S(1)} %get-tuple-element.19.small, f32[2,8,128]{2,1,0:T(8,128)S(1)} %get-tuple-element.20.columns, f32[16,2,8,8,128]{4,3,2,1,0:T(8,128)S(1)} %bitcast.16), custom_call_target="tpu_custom_call" | custom-call | flops 26214400 | bytes 1048576 | tf_op jit(solution)/shard_map/interior/pallas_call | solution.py:281
  10.3 2.8 %collective-permute-done.2.corner = f32[8,128]{1,0:T(8,128)S(1)} collective-permute-done((f32[8,128]{1,0:T(8,128)S(1)}, f32[8,128]{1,0:T(8,128)S(1)}, u32[]{:S(2)}, u32[]{:S(2)}) %collective-permute-start.2) | collective-permute-done | bytes 4128 | tf_op jit(solution)/shard_map/ppermute | solution.py:34
  13.1 0.0 collective-permute-done.plane
  13.1 0.0 collective-permute-done.1.row
  13.1 0.4 %boundary.1 = f32[2,2,8,8,128]{4,3,2,1,0:T(8,128)S(1)} custom-call(f32[16,2,8,8,128]{4,3,2,1,0:T(8,128)S(1)} %bitcast.17, f32[2,8,8,128]{3,2,1,0:T(8,128)S(1)} %collective-permute-done.plane, f32[16,8,128]{2,1,0:T(8,128)S(1)} %collective-permute-done.1.row, f32[8,128]{1,0:T(8,128)S(1)} %collective-permute-done.2.corner, ...), custom_call_target="tpu_custom_call" | custom-call | tf_op jit(solution)/shard_map/boundary/pallas_call | solution.py:296
  13.5 3.0 %collective-permute-start.3 = (f32[2,2,8,8,128]{4,3,2,1,0:T(8,128)S(1)}, f32[2,2,8,8,128]{4,3,2,1,0:T(8,128)S(1)}, u32[]{:S(2)}, u32[]{:S(2)}) collective-permute-start(f32[2,2,8,8,128]{4,3,2,1,0:T(8,128)S(1)} %boundary.1), channel_id=1, source_target_pairs={{0,4},{4,0},{8,12},{12,8},{16,20},{20,16},{24,28},{28,24},{1,5},{5... | collective-permute-start | bytes 393224 | tf_op jit(solution)/shard_map/ppermute | solution.py:309
  16.5 4.0 %collective-permute-done.3 = f32[2,2,8,8,128]{4,3,2,1,0:T(8,128)S(1)} collective-permute-done((f32[2,2,8,8,128]{4,3,2,1,0:T(8,128)S(1)}, f32[2,2,8,8,128]{4,3,2,1,0:T(8,128)S(1)}, u32[]{:S(2)}, u32[]{:S(2)}) %collective-permute-start.3) | collective-permute-done | bytes 131104 | tf_op jit(solution)/shard_map/ppermute | solution.py:309
  20.6 0.9 %collective-permute-start.4 = (f32[2,2,8,8,128]{4,3,2,1,0:T(8,128)S(1)}, f32[2,2,8,8,128]{4,3,2,1,0:T(8,128)S(1)}, u32[]{:S(2)}, u32[]{:S(2)}) collective-permute-start(f32[2,2,8,8,128]{4,3,2,1,0:T(8,128)S(1)} %pad_maximum_fusion), channel_id=1, source_target_pairs={{0,8},{4,12},{8,0},{12,4},{16,24},{20,28},{24,16},{28,20},{1,9},{5... | collective-permute-start | bytes 393224 | tf_op jit(solution)/shard_map/ppermute | solution.py:309
  21.5 4.7 %collective-permute-done.4 = f32[2,2,8,8,128]{4,3,2,1,0:T(8,128)S(1)} collective-permute-done((f32[2,2,8,8,128]{4,3,2,1,0:T(8,128)S(1)}, f32[2,2,8,8,128]{4,3,2,1,0:T(8,128)S(1)}, u32[]{:S(2)}, u32[]{:S(2)}) %collective-permute-start.4) | collective-permute-done | bytes 131104 | tf_op jit(solution)/shard_map/ppermute | solution.py:309
  26.3 3.7 %collective-permute-start.5 = (f32[2,2,8,8,128]{4,3,2,1,0:T(8,128)S(1)}, f32[2,2,8,8,128]{4,3,2,1,0:T(8,128)S(1)}, u32[]{:S(2)}, u32[]{:S(2)}) collective-permute-start(f32[2,2,8,8,128]{4,3,2,1,0:T(8,128)S(1)} %pad_maximum_fusion.1.state), channel_id=1, source_target_pairs={{0,24},{4,28},{8,16},{12,20},{16,8},{20,12},{24,0},{28,4},{1,25},{... | collective-permute-start | bytes 393224 | tf_op jit(solution)/shard_map/ppermute | solution.py:313
  29.9 3.8 %collective-permute-done.5.other = f32[2,2,8,8,128]{4,3,2,1,0:T(8,128)S(1)} collective-permute-done((f32[2,2,8,8,128]{4,3,2,1,0:T(8,128)S(1)}, f32[2,2,8,8,128]{4,3,2,1,0:T(8,128)S(1)}, u32[]{:S(2)}, u32[]{:S(2)}) %collective-permute-start.5) | collective-permute-done | bytes 131104 | tf_op jit(solution)/shard_map/ppermute | solution.py:313
  33.7 0.7 %last_merge.1 = (f32[1,2,8,8,128]{4,3,2,1,0:T(8,128)}, f32[2,2,8,8,128]{4,3,2,1,0:T(8,128)}) custom-call(f32[2,2,8,8,128]{4,3,2,1,0:T(8,128)S(1)} %pad_maximum_fusion.1.state, f32[2,2,8,8,128]{4,3,2,1,0:T(8,128)S(1)} %collective-permute-done.5.other, f32[1,2,8,8,128]{4,3,2,1,0:T(8,128)S(1)} %fusion.front), custom_call_target="tpu_custom_call" | custom-call | tf_op jit(solution)/shard_map/last_merge/pallas_call | solution.py:314
  (7 shorter events, 0.1 us)
Async XLA Ops:
  0.6 0.7 %copy-start.2 = (s32[1024]{0:T(1024)S(1)}, s32[1024]{0:T(1024)}, u32[]{:S(2)}) copy-start(s32[1024]{0:T(1024)} %param.12) | copy-start | bytes 12292
  0.6 0.7 %copy-start.6 = (s32[1,1,8]{2,1,0:T(1,128)S(1)}, s32[1,1,8]{2,1,0:T(1,128)}, u32[]{:S(2)}) copy-start(s32[1,1,8]{2,1,0:T(1,128)} %param.11) | copy-start | bytes 100
  0.7 0.7 %copy-start.7 = (s32[16]{0:T(128)S(1)}, s32[16]{0:T(128)}, u32[]{:S(2)}) copy-start(s32[16]{0:T(128)} %param.13) | copy-start | bytes 196
  0.7 0.7 %copy-start.3 = (s32[16]{0:T(128)S(1)}, s32[16]{0:T(128)}, u32[]{:S(2)}) copy-start(s32[16]{0:T(128)} %param.8) | copy-start | bytes 196
  0.7 0.7 %copy-start.4 = (f32[8]{0:T(128)S(1)}, f32[8]{0:T(128)}, u32[]{:S(2)}) copy-start(f32[8]{0:T(128)} %param.9) | copy-start | bytes 100
  0.7 0.7 %copy-start.5 = (f32[8]{0:T(128)S(1)}, f32[8]{0:T(128)}, u32[]{:S(2)}) copy-start(f32[8]{0:T(128)} %param.10) | copy-start | bytes 100
  1.4 1.2 %copy-start = (f32[16,16,1024]{2,1,0:T(8,128)S(1)}, f32[16,16,1024]{2,1,0:T(8,128)}, u32[]{:S(2)}) copy-start(f32[16,16,1024]{2,1,0:T(8,128)} %param.7) | copy-start | bytes 3145732
  2.6 4.3 %copy-start.1 = (f32[16,16,1024]{2,1,0:T(8,128)S(1)}, f32[16,16,1024]{2,1,0:T(8,128)}, u32[]{:S(2)}) copy-start(f32[16,16,1024]{2,1,0:T(8,128)} %param.7) | copy-start | bytes 3145732
  2.8 10.3 %collective-permute-start = (f32[2,8,8,128]{3,2,1,0:T(8,128)S(1)}, f32[2,8,8,128]{3,2,1,0:T(8,128)S(1)}, u32[]{:S(2)}, u32[]{:S(2)}) collective-permute-start(f32[2,8,8,128]{3,2,1,0:T(8,128)S(1)} %get-tuple-element.15), channel_id=1, source_target_pairs={{4,0},{8,4},{12,8},{16,12},{20,16},{24,20},{28,24},{5,1},{9,5},{13... | collective-permute-start | bytes 196616 | tf_op jit(solution)/shard_map/ppermute | solution.py:24
  4.3 8.8 %collective-permute-start.1 = (f32[16,8,128]{2,1,0:T(8,128)S(1)}, f32[16,8,128]{2,1,0:T(8,128)S(1)}, u32[]{:S(2)}, u32[]{:S(2)}) collective-permute-start(f32[16,8,128]{2,1,0:T(8,128)S(1)} %get-tuple-element.16), channel_id=1, source_target_pairs={{1,0},{2,1},{3,2},{5,4},{6,5},{7,6},{9,8},{10,9},{11,10},{13,12},{... | collective-permute-start | bytes 196616 | tf_op jit(solution)/shard_map/ppermute | solution.py:24
  5.6 7.5 %collective-permute-start.2 = (f32[8,128]{1,0:T(8,128)S(1)}, f32[8,128]{1,0:T(8,128)S(1)}, u32[]{:S(2)}, u32[]{:S(2)}) collective-permute-start(f32[8,128]{1,0:T(8,128)S(1)} %get-tuple-element.17), channel_id=1, source_target_pairs={{5,0},{6,1},{7,2},{9,4},{10,5},{11,6},{13,8},{14,9},{15,10},{17,12... | collective-permute-start | bytes 12296 | tf_op jit(solution)/shard_map/ppermute | solution.py:34
  13.5 7.0 %collective-permute-start.3 = (f32[2,2,8,8,128]{4,3,2,1,0:T(8,128)S(1)}, f32[2,2,8,8,128]{4,3,2,1,0:T(8,128)S(1)}, u32[]{:S(2)}, u32[]{:S(2)}) collective-permute-start(f32[2,2,8,8,128]{4,3,2,1,0:T(8,128)S(1)} %boundary.1), channel_id=1, source_target_pairs={{0,4},{4,0},{8,12},{12,8},{16,20},{20,16},{24,28},{28,24},{1,5},{5... | collective-permute-start | bytes 393224 | tf_op jit(solution)/shard_map/ppermute | solution.py:309
  20.6 5.6 %collective-permute-start.4 = (f32[2,2,8,8,128]{4,3,2,1,0:T(8,128)S(1)}, f32[2,2,8,8,128]{4,3,2,1,0:T(8,128)S(1)}, u32[]{:S(2)}, u32[]{:S(2)}) collective-permute-start(f32[2,2,8,8,128]{4,3,2,1,0:T(8,128)S(1)} %pad_maximum_fusion), channel_id=1, source_target_pairs={{0,8},{4,12},{8,0},{12,4},{16,24},{20,28},{24,16},{28,20},{1,9},{5... | collective-permute-start | bytes 393224 | tf_op jit(solution)/shard_map/ppermute | solution.py:309
  26.3 7.4 %collective-permute-start.5 = (f32[2,2,8,8,128]{4,3,2,1,0:T(8,128)S(1)}, f32[2,2,8,8,128]{4,3,2,1,0:T(8,128)S(1)}, u32[]{:S(2)}, u32[]{:S(2)}) collective-permute-start(f32[2,2,8,8,128]{4,3,2,1,0:T(8,128)S(1)} %pad_maximum_fusion.1.state), channel_id=1, source_target_pairs={{0,24},{4,28},{8,16},{12,20},{16,8},{20,12},{24,0},{28,4},{1,25},{... | collective-permute-start | bytes 393224 | tf_op jit(solution)/shard_map/ppermute | solution.py:313

commit v4 on v3

v4 whole, which is shorter than its diff:
```python
import functools
import math

import jax
import jax.numpy as jnp
from jax import lax
from jax.experimental import pallas as pl
from jax.experimental.pallas import tpu as pltpu
from jax.sharding import PartitionSpec as P

SUB, LANES = 8, 128
F32 = jnp.float32
VMEM = pl.BlockSpec(memory_space=pltpu.VMEM)
HBM = pl.BlockSpec(memory_space=pltpu.HBM)
EDGES_VMEM = 67_043_328 - (512 << 10)


def params(mib):
    return pltpu.CompilerParams(vmem_limit_bytes=mib << 20)


def from_behind(block, axis):
    size = lax.axis_size(axis)
    return lax.ppermute(block, axis, [((i + 1) % size, i) for i in range(size)])


def plane_from_behind(plane):
    depth, rows = lax.axis_size("depth"), lax.axis_size("rows")
    even = lax.ppermute(plane, "depth", [(i, i ^ 1) for i in range(depth)])
    route = []
    for d in range(depth):
        for r in range(rows):
            end = d in (0, depth - 1)
            e, q = (d, r ^ 1) if end else ((d + 1 if d % 2 else d - 1), r)
            route.append((e * rows + q, d * rows + r))
    odd = lax.ppermute(plane, ("depth", "rows"), route)
    return jnp.where(lax.axis_index("depth") % 2 == 0, even, odd)


def unless_last(axis):
    return jnp.where(lax.axis_index(axis) == lax.axis_size(axis) - 1, 0.0, 1.0)


def wide(row):
    return jnp.broadcast_to(row, (SUB, LANES))


def edges_kernel(density, *refs):
    small, (plane, row, last_row, *small_out), sems = refs[:6], refs[6:15], refs[15]
    height = density.shape[1]
    pieces = [
        (density.at[0], plane),
        (density.at[:, 0, :, 0, :], row),
        (density.at[:, height - 1, :, SUB - 1, :], last_row),
        *zip(small, small_out, strict=True),
    ]
    copies = [pltpu.make_async_copy(a, b, sems.at[i]) for i, (a, b) in enumerate(pieces)]
    for copy in copies:
        copy.start()
    for copy in copies:
        copy.wait()


def hats(values, table, levels):
    def at(k):
        return wide(table[k : k + 1, :])

    absorption = [at(0) + at(1) * u for u in values]
    emission = [at(levels) + at(levels + 1) * u for u in values]
    for k in range(1, levels - 1):
        gain_a, gain_e = at(k + 1), at(levels + k + 1)
        for j, u in enumerate(values):
            kink = jnp.maximum(u, float(k))
            absorption[j] = absorption[j] + gain_a * kink
            emission[j] = emission[j] + gain_e * kink
    return absorption, emission


def interior_kernel(
    bins, absorb_bins, emit_bins, occupied, row_offsets, col_offsets, density,
    state, last_state, table, masks, columns, rows, weights, scaled, small,
):
    planes, height, tiles = density.shape[:3]
    levels = bins.shape[1]
    small[...] = jnp.zeros_like(small)
    for i, source in enumerate((bins, absorb_bins, emit_bins, occupied, row_offsets)):
        small[i : i + 1, : source.shape[1]] = source[...].astype(F32)
    fraction = col_offsets[...].astype(F32) * 0.125
    shape = fraction.shape
    ends = (lax.broadcasted_iota(jnp.int32, shape, 0) == tiles - 1) & (
        lax.broadcasted_iota(jnp.int32, shape, 1) == LANES - 1
    )
    columns[0] = 1.0 - fraction
    columns[1] = jnp.where(ends, 0.0, fraction)
    lane = lax.broadcasted_iota(jnp.int32, (SUB, LANES), 1)
    sub = lax.broadcasted_iota(jnp.int32, (SUB, LANES), 0)
    lane_end, row_end = lane == LANES - 1, sub == SUB - 1
    bins, absorb_bins, emit_bins, occupied, row_offsets = (
        wide(small[i : i + 1, :]) for i in range(5)
    )

    def pick(vector, k):
        return jnp.broadcast_to(vector[:, k : k + 1], (SUB, LANES))

    scale = 0.5 * (levels - 1)
    near, far = [], []
    for r in range(height):
        offset = jnp.zeros((SUB, LANES), F32)
        for i in range(SUB):
            offset = jnp.where(sub == i, pick(row_offsets, r * SUB + i), offset)
        far.append(offset * (scale / 8.0))
        near.append(scale - far[r])
        weights[0, r] = near[r]
        weights[1, r] = far[r]
    rows[0:1, :] = near[-1][SUB - 1 :, :]
    rows[1:2, :] = far[-1][SUB - 1 :, :]
    for t in range(tiles):
        masks[t : t + 1, :] = pick(occupied, t)[:1, :]

    which = bins.astype(jnp.int32)
    for first, level, unit in ((0, absorb_bins, -1.0 / math.log(2.0)), (levels, emit_bins, 1.0)):
        value = jnp.take_along_axis(level, which, axis=1, mode="promise_in_bounds") * unit
        slope = pltpu.roll(value, LANES - 1, 1) - value
        gain = jnp.where(lane == 0, slope, slope - pltpu.roll(slope, 1, 1))
        shift = jnp.where(lane < levels - 1, gain * lane.astype(F32), 0.0)
        base = pick(value, 0) - jnp.sum(shift, 1, keepdims=True)
        table[first : first + 1, :] = base[:1, :]
        for k in range(levels - 1):
            table[first + k + 1 : first + k + 2, :] = pick(gain, k)[:1, :]

    for z in range(planes - 1):

        def mixed(t):
            mid = [density[z, r, t] + density[z + 1, r, t] for r in range(height)]
            up = [pltpu.roll(m, SUB - 1, 0) for m in mid]
            below = [
                jnp.where(row_end, up[r + 1], up[r]) if r + 1 < height else up[r]
                for r in range(height)
            ]
            return [near[r] * mid[r] + far[r] * below[r] for r in range(height)]

        now = mixed(0)
        turned = [pltpu.roll(m, LANES - 1, 1) for m in now]
        for t in range(tiles):
            if t + 1 < tiles:
                after = mixed(t + 1)
                after_turned = [pltpu.roll(m, LANES - 1, 1) for m in after]
            else:
                after, after_turned = now, turned
            left, right = columns[0, t : t + 1, :], columns[1, t : t + 1, :]
            for r in range(height):
                beside = jnp.where(lane_end, after_turned[r], turned[r])
                scaled[z, r, t] = left * now[r] + right * beside
            now, turned = after, after_turned

    @pl.loop(0, tiles)
    def _(t):
        mask = wide(masks[pl.ds(t, 1), :])
        total = [jnp.zeros((SUB, LANES), F32)] * height
        through = [jnp.ones((SUB, LANES), F32)] * height
        light = [jnp.zeros((SUB, LANES), F32)] * height
        for z in range(planes - 1):
            absorption, emission = hats([scaled[z, r, t] for r in range(height)], table, levels)
            for r in range(height):
                total[r] = total[r] + absorption[r] * mask
                behind = jnp.exp2(total[r])
                light[r] = light[r] + (through[r] - behind) * emission[r]
                through[r] = behind
        for r in range(height - 1):
            state[0, r, t] = light[r]
            state[1, r, t] = through[r]
        last_state[0, 0, t] = light[-1]
        last_state[1, 0, t] = through[-1]


def add_last_plane(density, plane, table, masks, columns, weights, before, state, tiles_of_rows):
    planes, height, tiles = density.shape[:3]
    levels = table.shape[0] // 2
    some = unless_last("depth")
    lane_end = lax.broadcasted_iota(jnp.int32, (SUB, LANES), 1) == LANES - 1
    row_end = lax.broadcasted_iota(jnp.int32, (SUB, LANES), 0) == SUB - 1
    value = []
    for r in tiles_of_rows:
        line = []
        for t in range(tiles):
            mid = density[planes - 1, r, t] + some * plane[r, t]
            below = pltpu.roll(mid, SUB - 1, 0)
            if r + 1 < height:
                next_mid = density[planes - 1, r + 1, t] + some * plane[r + 1, t]
                below = jnp.where(row_end, pltpu.roll(next_mid, SUB - 1, 0), below)
            line.append(weights[0, r] * mid + weights[1, r] * below)
        turned = [pltpu.roll(m, LANES - 1, 1) for m in line]
        for t in range(tiles):
            beside = jnp.where(lane_end, turned[min(t + 1, tiles - 1)], turned[t])
            value.append(columns[0, t : t + 1, :] * line[t] + columns[1, t : t + 1, :] * beside)
    group = 4
    count = len(value)
    for first in range(0, count, group):
        absorption, emission = hats(value[first : first + group], table, levels)
        for j, (a, e) in enumerate(zip(absorption, emission, strict=True), first):
            i, t = divmod(j, tiles)
            through = before[1, i, t]
            behind = through * jnp.exp2(a * wide(masks[t : t + 1, :]))
            state[0, i, t] = before[0, i, t] + (through - behind) * e
            state[1, i, t] = behind


def upper_kernel(
    density, plane, row, table, masks, columns, weights, before, state, row_sums
):
    planes, height, tiles = density.shape[:3]
    for z in range(planes - 1):
        row_sums[z] = row[z] + row[z + 1]
    after = jnp.concatenate([plane[0, t, :1, :] for t in range(tiles)], 0)
    row_sums[planes - 1] = row[planes - 1] + unless_last("depth") * after
    add_last_plane(
        density, plane, table, masks, columns, weights, before, state, range(height - 1)
    )


def lower_kernel(
    density, plane, below, last_row, table, masks, columns, rows, weights, before, state
):
    planes, height, tiles = density.shape[:3]
    levels = table.shape[0] // 2
    add_last_plane(density, plane, table, masks, columns, weights, before, state, [height - 1])

    shape = (tiles, LANES)
    fold_end = lax.broadcasted_iota(jnp.int32, shape, 1) == LANES - 1
    near, far = rows[0:1, :], unless_last("rows") * rows[1:2, :]
    left, right = columns[0], columns[1]
    after = jnp.concatenate([plane[height - 1, t, SUB - 1 :, :] for t in range(tiles)], 0)
    own = [last_row[z] for z in range(planes)] + [unless_last("depth") * after]
    value = []
    for z in range(planes):
        line = near * (own[z] + own[z + 1]) + far * below[z]
        turned = pltpu.roll(line, LANES - 1, 1)
        beside = jnp.where(fold_end, pltpu.roll(turned, tiles - 1, 0), turned)
        value.append(left * line + right * beside)
    total = jnp.zeros(shape, F32)
    through = jnp.ones(shape, F32)
    light = jnp.zeros(shape, F32)
    group = 4
    for first in range(0, planes, group):
        absorption, emission = hats(value[first : first + group], table, levels)
        for a, e in zip(absorption, emission, strict=True):
            total = total + a * masks[...]
            behind = jnp.exp2(total)
            light = light + (through - behind) * e
            through = behind
    for t in range(tiles):
        state[0, 0, t, SUB - 1 :, :] = light[t : t + 1, :]
        state[1, 0, t, SUB - 1 :, :] = through[t : t + 1, :]


def is_behind(step):
    return (lax.axis_index("depth") & step) != 0


def merge(state, other, front, step):
    behind = is_behind(step)
    first = jnp.where(behind, other, state)
    second = jnp.where(behind, state, other)
    front = front * jnp.where(behind, other[1:], 1.0)
    return jnp.stack([first[0] + first[1] * second[0], first[1] * second[1]]), front


def last_merge_kernel(*refs, step, parts):
    ins, (front_out, image_out, front_buf, image_buf, sems) = refs[: 3 * parts], refs[3 * parts :]
    behind = is_behind(step)
    first, copies = 0, []
    for part in range(parts):
        state, other, front = ins[3 * part : 3 * part + 3]
        at = pl.ds(first, state.shape[1])
        first += state.shape[1]
        light, through = state[0], state[1]
        other_light, other_through = other[0], other[1]
        front_buf[0, at] = front[0] * jnp.where(behind, other_through, 1.0)
        image_buf[0, at] = jnp.where(
            behind, other_light + other_through * light, light + through * other_light
        )
        image_buf[1, at] = through * other_through
        copies += [
            pltpu.make_async_copy(front_buf.at[:, at], front_out.at[:, at], sems.at[2 * part]),
            pltpu.make_async_copy(image_buf.at[:, at], image_out.at[:, at], sems.at[2 * part + 1]),
        ]
        copies[-2].start()
        copies[-1].start()
    for copy in copies:
        copy.wait()


def on_device(density, bin_of_level, absorb_bins, emit_bins, occupancy, col_offsets, row_offsets):
    planes, rows, cols = density.shape
    height, tiles = rows // SUB, cols // LANES
    levels = bin_of_level.shape[0]
    tiled = density.reshape(planes, height, SUB, tiles, LANES).transpose(0, 1, 3, 2, 4)
    flat = (height, tiles, SUB, LANES)
    upper = (2, height - 1, tiles, SUB, LANES)
    lower = (2, 1, tiles, SUB, LANES)

    def out(*shape):
        return jax.ShapeDtypeStruct(shape, F32)

    small = (
        bin_of_level[None], absorb_bins[None], emit_bins[None], occupancy.reshape(1, tiles),
        row_offsets[None], col_offsets.reshape(tiles, LANES),
    )
    plane, row, last_row, *small = pl.pallas_call(
        edges_kernel,
        out_shape=[
            out(*flat), out(planes, tiles, LANES), out(planes, tiles, LANES),
            *[jax.ShapeDtypeStruct(x.shape, x.dtype) for x in small],
        ],
        in_specs=[HBM] * 7,
        out_specs=[VMEM] * 9,
        scratch_shapes=[pltpu.SemaphoreType.DMA((9,))],
        compiler_params=params(2),
        name="edges",
    )(*[pltpu.with_memory_space_constraint(x, pltpu.HBM) for x in (tiled, *small)])
    plane = plane_from_behind(plane)

    work = density.size
    above, under, table, masks, columns, last_weights, weights = pl.pallas_call(
        interior_kernel,
        out_shape=[
            out(*upper), out(*lower), out(2 * levels, LANES), out(tiles, LANES),
            out(2, tiles, LANES), out(2, LANES), out(2, height, SUB, LANES),
        ],
        in_specs=[VMEM] * 7,
        out_specs=[VMEM] * 7,
        scratch_shapes=[pltpu.VMEM((planes - 1, *flat), F32), pltpu.VMEM((SUB, LANES), F32)],
        cost_estimate=pl.CostEstimate(
            flops=100 * work, bytes_accessed=4 * work, transcendentals=work
        ),
        compiler_params=params(8),
        name="interior",
    )(*small, tiled)
    above, row = pl.pallas_call(
        upper_kernel,
        out_shape=[out(*upper), out(planes, tiles, LANES)],
        in_specs=[VMEM] * 8,
        out_specs=[VMEM] * 2,
        compiler_params=params(8),
        name="upper",
    )(tiled, plane, row, table, masks, columns, weights, above)
    row = from_behind(row, "rows")
    under = pl.pallas_call(
        lower_kernel,
        out_shape=out(*lower),
        in_specs=[VMEM] * 10,
        out_specs=VMEM,
        cost_estimate=pl.CostEstimate(
            flops=10 * work, bytes_accessed=work, transcendentals=work // 8
        ),
        compiler_params=params(8),
        name="lower",
    )(tiled, plane, row, last_row, table, masks, columns, last_weights, weights, under)

    size = lax.axis_size("depth")
    states = [above, under]
    fronts = [jnp.ones((1, *part.shape[1:]), F32) for part in states]
    step = 1
    while 2 * step < size:
        route = [(i, i ^ step) for i in range(size)]
        others = [lax.ppermute(state, "depth", route) for state in states]
        merged = [
            merge(state, other, front, step)
            for state, other, front in zip(states, others, fronts, strict=True)
        ]
        states, fronts = zip(*merged, strict=True)
        step *= 2
    route = [(i, i ^ step) for i in range(size)]
    others = [lax.ppermute(state, "depth", route) for state in states]
    parts = len(states)
    front, image = pl.pallas_call(
        functools.partial(last_merge_kernel, step=step, parts=parts),
        out_shape=[out(1, *flat), out(2, *flat)],
        in_specs=[VMEM] * (3 * parts),
        out_specs=[HBM] * 2,
        scratch_shapes=[
            pltpu.VMEM((1, *flat), F32),
            pltpu.VMEM((2, *flat), F32),
            pltpu.SemaphoreType.DMA((2 * parts,)),
        ],
        compiler_params=params(4),
        name="last_merge",
    )(*[ref for group in zip(states, others, fronts, strict=True) for ref in group])

    def plain(block):
        return block.transpose(0, 1, 3, 2, 4).reshape(-1, rows, cols)

    return (plain(front), plain(image))


def solution(mesh):
    placed = (P("depth", "rows", None), P(), P(), P(), P("depth", "rows", None), P(), P("rows"))
    return jax.shard_map(
        on_device,
        mesh=mesh,
        in_specs=placed,
        out_specs=(P("depth", "rows", None), P(None, "rows", None)),
        check_vma=False,
    )
```

time: 34.7 us -> 28.5 us (0.82)
  waiting for transfers between devices: 15.3 us -> 3.99 us
  starting transfers between devices: 11.6 us -> 17.7 us
  local copies, waits for them, and re-layouts: 1.91 us -> 0.01 us
  Pallas kernels: 4.76 us -> 5.71 us
    ppermute x6 -> x9, waiting for transfers between devices: 15.3 us -> 3.99 us  [the longest x6 3.68 us: on_device(): others = [lax.ppermute(state, 'depth', route) for state in states]]
    ppermute x6 -> x9, starting transfers between devices: 11.6 us -> 17.7 us  [the longest x6 12.7 us: on_device(): others = [lax.ppermute(state, 'depth', route) for state in states]]
    unnamed x16 -> x2, local copies, waits for them, and re-layouts: 1.91 us -> 0.01 us
    pallas_call x1, Pallas kernels: 0.22 us -> 1.09 us  [on_device(): pl.pallas_call(edges_kernel, out_shape=[out(*flat), out(planes, tiles, LA...]
    pallas_call x3 -> x4, Pallas kernels: 4.54 us -> 4.62 us  [the longest x1 3.36 us: on_device(): pl.pallas_call(interior_kernel, out_shape=[out(*upper), out(*lower), out(...]
  transfers between devices with their start and end apart: 6 -> 9, of which waited for: 4 -> 5; matrix products, arithmetic and copies ran while one was open for 0% -> 1% of each run, Pallas kernels for 10% -> 13%
where the time goes in v4:
time: 28.5 us; the launch traced here: 28.3 us
  starting transfers between devices  17.7 us (62%)
  Pallas kernels  5.71 us (20%)
  waiting for transfers between devices  3.99 us (14%)
  between operations  0.78 us (3%)
    ppermute x6, starting transfers between devices, on_device(): others = [lax.ppermute(state, 'depth', route) for state in states]  12.7 us
    ppermute x1, starting transfers between devices, plane_from_behind(): even = lax.ppermute(plane, 'depth', [(i, i ^ 1) for i in range(depth)])  4.02 us
    ppermute x6, waiting for transfers between devices, on_device(): others = [lax.ppermute(state, 'depth', route) for state in states]  3.68 us
    pallas_call x1, Pallas kernels, on_device(): pl.pallas_call(interior_kernel, out_shape=[out(*upper), out(*lower), out(...  3.36 us
    pallas_call x1, Pallas kernels, on_device(): pl.pallas_call(edges_kernel, out_shape=[out(*flat), out(planes, tiles, LA...  1.09 us
    pallas_call x1, Pallas kernels, on_device(): pl.pallas_call(functools.partial(last_merge_kernel, step=step, parts=part...  0.72 us
  transfers between devices with their start and end apart: 9, of which 5 were waited for; matrix products, arithmetic and copies ran while one was open for 1% of the time, Pallas kernels for 13%

profile of v4, /device:TPU:0, one launch (start us, length us, event | category | flops | bytes accessed | tf_op | source)
XLA Modules:
  0.0 28.3 jit_solution(1221534464597996257)
XLA Ops:
  0.6 0.0 copy-start
  0.6 1.1 %edges.1 = (f32[2,8,8,128]{3,2,1,0:T(8,128)S(1)}, f32[16,8,128]{2,1,0:T(8,128)S(1)}, f32[16,8,128]{2,1,0:T(8,128)S(1)}, s32[1,16]{1,0:T(1,128)S(1)}, f32[1,8]{1,...) custom-call(f32[16,2,8,8,128]{4,3,2,1,0:T(8,128)} %bitcast.15, ...), custom_call_target="tpu_custom_call" | custom-call | tf_op jit(solution)/shard_map/edges/pallas_call | solution.py:309
  1.7 0.6 %collective-permute-start.1 = (f32[2,8,8,128]{3,2,1,0:T(8,128)S(1)}, f32[2,8,8,128]{3,2,1,0:T(8,128)S(1)}, u32[]{:S(2)}, u32[]{:S(2)}) collective-permute-start(f32[2,8,8,128]{3,2,1,0:T(8,128)S(1)} %get-tuple-element.22), channel_id=1, source_target_pairs={{1,0},{0,1},{3,2},{2,3},{8,4},{9,5},{10,6},{11,7},{4,8},{5,9},{6,1... | collective-permute-start | bytes 196616 | tf_op jit(solution)/shard_map/ppermute | solution.py:36
  2.3 4.0 %collective-permute-start = (f32[2,8,8,128]{3,2,1,0:T(8,128)S(1)}, f32[2,8,8,128]{3,2,1,0:T(8,128)S(1)}, u32[]{:S(2)}, u32[]{:S(2)}) collective-permute-start(f32[2,8,8,128]{3,2,1,0:T(8,128)S(1)} %get-tuple-element.22), channel_id=1, source_target_pairs={{0,4},{4,0},{8,12},{12,8},{16,20},{20,16},{24,28},{28,24},{1,5},{5... | collective-permute-start | bytes 196616 | tf_op jit(solution)/shard_map/ppermute | solution.py:29
  6.3 0.0 copy-done
  6.3 3.4 %interior.1 = (f32[2,1,8,8,128]{4,3,2,1,0:T(8,128)S(1)}, f32[2,1,8,8,128]{4,3,2,1,0:T(8,128)S(1)}, f32[32,128]{1,0:T(8,128)S(1)}, f32[8,128]{1,0:T(8,128)S(1)}, ...) custom-call(s32[1,16]{1,0:T(1,128)S(1)} %get-tuple-element.24.bins, ...), custom_call_target="tpu_custom_call" | custom-call | flops 26214400 | bytes 1048576 | tf_op jit(solution)/shard_map/interior/pallas_call | solution.py:324
  9.7 0.0 collective-permute-done.1
  9.7 0.0 collective-permute-done
  9.7 0.2 upper.1
  9.9 0.5 %collective-permute-start.5 = (f32[16,8,128]{2,1,0:T(8,128)S(1)}, f32[16,8,128]{2,1,0:T(8,128)S(1)}, u32[]{:S(2)}, u32[]{:S(2)}) collective-permute-start(f32[16,8,128]{2,1,0:T(8,128)S(1)} %get-tuple-element.36), channel_id=1, source_target_pairs={{1,0},{2,1},{3,2},{0,3},{5,4},{6,5},{7,6},{4,7},{9,8},{10,9},{11,1... | collective-permute-start | bytes 196616 | tf_op jit(solution)/shard_map/ppermute | solution.py:24
  10.4 1.6 %collective-permute-start.2 = (f32[2,1,8,8,128]{4,3,2,1,0:T(8,128)S(1)}, f32[2,1,8,8,128]{4,3,2,1,0:T(8,128)S(1)}, u32[]{:S(2)}, u32[]{:S(2)}) collective-permute-start(f32[2,1,8,8,128]{4,3,2,1,0:T(8,128)S(1)} %get-tuple-element.35), channel_id=1, source_target_pairs={{0,4},{4,0},{8,12},{12,8},{16,20},{20,16},{24,28},{28,24},{1,5},{5... | collective-permute-start | bytes 196616 | tf_op jit(solution)/shard_map/ppermute | solution.py:366
  12.0 0.3 %collective-permute-done.5.below = f32[16,8,128]{2,1,0:T(8,128)S(1)} collective-permute-done((f32[16,8,128]{2,1,0:T(8,128)S(1)}, f32[16,8,128]{2,1,0:T(8,128)S(1)}, u32[]{:S(2)}, u32[]{:S(2)}) %collective-permute-start.5) | collective-permute-done | bytes 65568 | tf_op jit(solution)/shard_map/ppermute | solution.py:24
  12.3 0.4 %lower.1 = f32[2,1,8,8,128]{4,3,2,1,0:T(8,128)S(1)} custom-call(f32[16,2,8,8,128]{4,3,2,1,0:T(8,128)S(1)} %bitcast.18, f32[2,8,8,128]{3,2,1,0:T(8,128)S(1)} %broadcast_select_fusion.plane, f32[16,8,128]{2,1,0:T(8,128)S(1)} %collective-permute-done.5.below, f32[16,8,128]{2,1,0:T(8,128)S(1)} %get-tuple-element.37.last_row, ...), custom_call_target="tpu_custom_call" | custom-call | flops 2621440 | bytes 262144 | tf_op jit(solution)/shard_map/lower/pallas_call | solution.py:348
  12.6 1.7 %collective-permute-start.6 = (f32[2,1,8,8,128]{4,3,2,1,0:T(8,128)S(1)}, f32[2,1,8,8,128]{4,3,2,1,0:T(8,128)S(1)}, u32[]{:S(2)}, u32[]{:S(2)}) collective-permute-start(f32[2,1,8,8,128]{4,3,2,1,0:T(8,128)S(1)} %lower.1), channel_id=1, source_target_pairs={{0,4},{4,0},{8,12},{12,8},{16,20},{20,16},{24,28},{28,24},{1,5},{5... | collective-permute-start | bytes 196616 | tf_op jit(solution)/shard_map/ppermute | solution.py:366
  14.3 0.3 %collective-permute-done.2 = f32[2,1,8,8,128]{4,3,2,1,0:T(8,128)S(1)} collective-permute-done((f32[2,1,8,8,128]{4,3,2,1,0:T(8,128)S(1)}, f32[2,1,8,8,128]{4,3,2,1,0:T(8,128)S(1)}, u32[]{:S(2)}, u32[]{:S(2)}) %collective-permute-start.2) | collective-permute-done | bytes 65568 | tf_op jit(solution)/shard_map/ppermute | solution.py:366
  14.7 1.7 %collective-permute-start.3 = (f32[2,1,8,8,128]{4,3,2,1,0:T(8,128)S(1)}, f32[2,1,8,8,128]{4,3,2,1,0:T(8,128)S(1)}, u32[]{:S(2)}, u32[]{:S(2)}) collective-permute-start(f32[2,1,8,8,128]{4,3,2,1,0:T(8,128)S(1)} %pad_maximum_fusion), channel_id=1, source_target_pairs={{0,8},{4,12},{8,0},{12,4},{16,24},{20,28},{24,16},{28,20},{1,9},{5... | collective-permute-start | bytes 196616 | tf_op jit(solution)/shard_map/ppermute | solution.py:366
  16.4 0.9 %collective-permute-done.6 = f32[2,1,8,8,128]{4,3,2,1,0:T(8,128)S(1)} collective-permute-done((f32[2,1,8,8,128]{4,3,2,1,0:T(8,128)S(1)}, f32[2,1,8,8,128]{4,3,2,1,0:T(8,128)S(1)}, u32[]{:S(2)}, u32[]{:S(2)}) %collective-permute-start.6) | collective-permute-done | bytes 65568 | tf_op jit(solution)/shard_map/ppermute | solution.py:366
  17.4 1.8 %collective-permute-start.7 = (f32[2,1,8,8,128]{4,3,2,1,0:T(8,128)S(1)}, f32[2,1,8,8,128]{4,3,2,1,0:T(8,128)S(1)}, u32[]{:S(2)}, u32[]{:S(2)}) collective-permute-start(f32[2,1,8,8,128]{4,3,2,1,0:T(8,128)S(1)} %pad_maximum_fusion.2), channel_id=1, source_target_pairs={{0,8},{4,12},{8,0},{12,4},{16,24},{20,28},{24,16},{28,20},{1,9},{5... | collective-permute-start | bytes 196616 | tf_op jit(solution)/shard_map/ppermute | solution.py:366
  19.3 0.0 collective-permute-done.3
  19.3 2.8 %collective-permute-start.4 = (f32[2,1,8,8,128]{4,3,2,1,0:T(8,128)S(1)}, f32[2,1,8,8,128]{4,3,2,1,0:T(8,128)S(1)}, u32[]{:S(2)}, u32[]{:S(2)}) collective-permute-start(f32[2,1,8,8,128]{4,3,2,1,0:T(8,128)S(1)} %pad_maximum_fusion.1.refs_0_), channel_id=1, source_target_pairs={{0,16},{4,20},{8,24},{12,28},{16,0},{20,4},{24,8},{28,12},{1,17},{... | collective-permute-start | bytes 196616 | tf_op jit(solution)/shard_map/ppermute | solution.py:374
  22.1 0.0 collective-permute-done.7
  22.1 3.1 %collective-permute-start.8 = (f32[2,1,8,8,128]{4,3,2,1,0:T(8,128)S(1)}, f32[2,1,8,8,128]{4,3,2,1,0:T(8,128)S(1)}, u32[]{:S(2)}, u32[]{:S(2)}) collective-permute-start(f32[2,1,8,8,128]{4,3,2,1,0:T(8,128)S(1)} %pad_maximum_fusion.3.refs_3_), channel_id=1, source_target_pairs={{0,16},{4,20},{8,24},{12,28},{16,0},{20,4},{24,8},{28,12},{1,17},{... | collective-permute-start | bytes 196616 | tf_op jit(solution)/shard_map/ppermute | solution.py:374
  25.2 1.1 %collective-permute-done.4.refs_1_ = f32[2,1,8,8,128]{4,3,2,1,0:T(8,128)S(1)} collective-permute-done((f32[2,1,8,8,128]{4,3,2,1,0:T(8,128)S(1)}, f32[2,1,8,8,128]{4,3,2,1,0:T(8,128)S(1)}, u32[]{:S(2)}, u32[]{:S(2)}) %collective-permute-start.4) | collective-permute-done | bytes 65568 | tf_op jit(solution)/shard_map/ppermute | solution.py:374
  26.3 1.3 %collective-permute-done.8.refs_4_ = f32[2,1,8,8,128]{4,3,2,1,0:T(8,128)S(1)} collective-permute-done((f32[2,1,8,8,128]{4,3,2,1,0:T(8,128)S(1)}, f32[2,1,8,8,128]{4,3,2,1,0:T(8,128)S(1)}, u32[]{:S(2)}, u32[]{:S(2)}) %collective-permute-start.8) | collective-permute-done | bytes 65568 | tf_op jit(solution)/shard_map/ppermute | solution.py:374
  27.6 0.7 %last_merge.1 = (f32[1,2,8,8,128]{4,3,2,1,0:T(8,128)}, f32[2,2,8,8,128]{4,3,2,1,0:T(8,128)}) custom-call(f32[2,1,8,8,128]{4,3,2,1,0:T(8,128)S(1)} %pad_maximum_fusion.1.refs_0_, f32[2,1,8,8,128]{4,3,2,1,0:T(8,128)S(1)} %collective-permute-done.4.refs_1_, f32[1,1,8,8,128]{4,3,2,1,0:T(8,128)S(1)} %fusion.3.refs_2_, ...), custom_call_target="tpu_custom_call" | custom-call | tf_op jit(solution)/shard_map/last_merge/pallas_call | solution.py:376
  (15 shorter events, 0.2 us)
Async XLA Ops:
  0.6 5.7 %copy-start = (f32[16,16,1024]{2,1,0:T(8,128)S(1)}, f32[16,16,1024]{2,1,0:T(8,128)}, u32[]{:S(2)}) copy-start(f32[16,16,1024]{2,1,0:T(8,128)} %param.7) | copy-start | bytes 3145732
  1.7 8.0 %collective-permute-start.1 = (f32[2,8,8,128]{3,2,1,0:T(8,128)S(1)}, f32[2,8,8,128]{3,2,1,0:T(8,128)S(1)}, u32[]{:S(2)}, u32[]{:S(2)}) collective-permute-start(f32[2,8,8,128]{3,2,1,0:T(8,128)S(1)} %get-tuple-element.22), channel_id=1, source_target_pairs={{1,0},{0,1},{3,2},{2,3},{8,4},{9,5},{10,6},{11,7},{4,8},{5,9},{6,1... | collective-permute-start | bytes 196616 | tf_op jit(solution)/shard_map/ppermute | solution.py:36
  2.3 7.4 %collective-permute-start = (f32[2,8,8,128]{3,2,1,0:T(8,128)S(1)}, f32[2,8,8,128]{3,2,1,0:T(8,128)S(1)}, u32[]{:S(2)}, u32[]{:S(2)}) collective-permute-start(f32[2,8,8,128]{3,2,1,0:T(8,128)S(1)} %get-tuple-element.22), channel_id=1, source_target_pairs={{0,4},{4,0},{8,12},{12,8},{16,20},{20,16},{24,28},{28,24},{1,5},{5... | collective-permute-start | bytes 196616 | tf_op jit(solution)/shard_map/ppermute | solution.py:29
  9.9 2.4 %collective-permute-start.5 = (f32[16,8,128]{2,1,0:T(8,128)S(1)}, f32[16,8,128]{2,1,0:T(8,128)S(1)}, u32[]{:S(2)}, u32[]{:S(2)}) collective-permute-start(f32[16,8,128]{2,1,0:T(8,128)S(1)} %get-tuple-element.36), channel_id=1, source_target_pairs={{1,0},{2,1},{3,2},{0,3},{5,4},{6,5},{7,6},{4,7},{9,8},{10,9},{11,1... | collective-permute-start | bytes 196616 | tf_op jit(solution)/shard_map/ppermute | solution.py:24
  10.4 4.3 %collective-permute-start.2 = (f32[2,1,8,8,128]{4,3,2,1,0:T(8,128)S(1)}, f32[2,1,8,8,128]{4,3,2,1,0:T(8,128)S(1)}, u32[]{:S(2)}, u32[]{:S(2)}) collective-permute-start(f32[2,1,8,8,128]{4,3,2,1,0:T(8,128)S(1)} %get-tuple-element.35), channel_id=1, source_target_pairs={{0,4},{4,0},{8,12},{12,8},{16,20},{20,16},{24,28},{28,24},{1,5},{5... | collective-permute-start | bytes 196616 | tf_op jit(solution)/shard_map/ppermute | solution.py:366
  12.6 4.7 %collective-permute-start.6 = (f32[2,1,8,8,128]{4,3,2,1,0:T(8,128)S(1)}, f32[2,1,8,8,128]{4,3,2,1,0:T(8,128)S(1)}, u32[]{:S(2)}, u32[]{:S(2)}) collective-permute-start(f32[2,1,8,8,128]{4,3,2,1,0:T(8,128)S(1)} %lower.1), channel_id=1, source_target_pairs={{0,4},{4,0},{8,12},{12,8},{16,20},{20,16},{24,28},{28,24},{1,5},{5... | collective-permute-start | bytes 196616 | tf_op jit(solution)/shard_map/ppermute | solution.py:366
  14.7 4.6 %collective-permute-start.3 = (f32[2,1,8,8,128]{4,3,2,1,0:T(8,128)S(1)}, f32[2,1,8,8,128]{4,3,2,1,0:T(8,128)S(1)}, u32[]{:S(2)}, u32[]{:S(2)}) collective-permute-start(f32[2,1,8,8,128]{4,3,2,1,0:T(8,128)S(1)} %pad_maximum_fusion), channel_id=1, source_target_pairs={{0,8},{4,12},{8,0},{12,4},{16,24},{20,28},{24,16},{28,20},{1,9},{5... | collective-permute-start | bytes 196616 | tf_op jit(solution)/shard_map/ppermute | solution.py:366
  17.4 4.7 %collective-permute-start.7 = (f32[2,1,8,8,128]{4,3,2,1,0:T(8,128)S(1)}, f32[2,1,8,8,128]{4,3,2,1,0:T(8,128)S(1)}, u32[]{:S(2)}, u32[]{:S(2)}) collective-permute-start(f32[2,1,8,8,128]{4,3,2,1,0:T(8,128)S(1)} %pad_maximum_fusion.2), channel_id=1, source_target_pairs={{0,8},{4,12},{8,0},{12,4},{16,24},{20,28},{24,16},{28,20},{1,9},{5... | collective-permute-start | bytes 196616 | tf_op jit(solution)/shard_map/ppermute | solution.py:366
  19.3 7.0 %collective-permute-start.4 = (f32[2,1,8,8,128]{4,3,2,1,0:T(8,128)S(1)}, f32[2,1,8,8,128]{4,3,2,1,0:T(8,128)S(1)}, u32[]{:S(2)}, u32[]{:S(2)}) collective-permute-start(f32[2,1,8,8,128]{4,3,2,1,0:T(8,128)S(1)} %pad_maximum_fusion.1.refs_0_), channel_id=1, source_target_pairs={{0,16},{4,20},{8,24},{12,28},{16,0},{20,4},{24,8},{28,12},{1,17},{... | collective-permute-start | bytes 196616 | tf_op jit(solution)/shard_map/ppermute | solution.py:374
  22.1 5.5 %collective-permute-start.8 = (f32[2,1,8,8,128]{4,3,2,1,0:T(8,128)S(1)}, f32[2,1,8,8,128]{4,3,2,1,0:T(8,128)S(1)}, u32[]{:S(2)}, u32[]{:S(2)}) collective-permute-start(f32[2,1,8,8,128]{4,3,2,1,0:T(8,128)S(1)} %pad_maximum_fusion.3.refs_3_), channel_id=1, source_target_pairs={{0,16},{4,20},{8,24},{12,28},{16,0},{20,4},{24,8},{28,12},{1,17},{... | collective-permute-start | bytes 196616 | tf_op jit(solution)/shard_map/ppermute | solution.py:374

commit v5 on v4

--- a/solution.py
+++ b/solution.py
@@ -12,7 +12,7 @@
 F32 = jnp.float32
 VMEM = pl.BlockSpec(memory_space=pltpu.VMEM)
 HBM = pl.BlockSpec(memory_space=pltpu.HBM)
-EDGES_VMEM = 67_043_328 - (512 << 10)
+SPAN = 5
 
 
 def params(mib):
@@ -26,7 +26,6 @@
 
 def plane_from_behind(plane):
     depth, rows = lax.axis_size("depth"), lax.axis_size("rows")
-    even = lax.ppermute(plane, "depth", [(i, i ^ 1) for i in range(depth)])
     route = []
     for d in range(depth):
         for r in range(rows):
@@ -34,6 +33,7 @@
             e, q = (d, r ^ 1) if end else ((d + 1 if d % 2 else d - 1), r)
             route.append((e * rows + q, d * rows + r))
     odd = lax.ppermute(plane, ("depth", "rows"), route)
+    even = lax.ppermute(plane, "depth", [(i, i ^ 1) for i in range(depth)])
     return jnp.where(lax.axis_index("depth") % 2 == 0, even, odd)
 
 
@@ -46,14 +46,8 @@
 
 
 def edges_kernel(density, *refs):
-    small, (plane, row, last_row, *small_out), sems = refs[:6], refs[6:15], refs[15]
-    height = density.shape[1]
-    pieces = [
-        (density.at[0], plane),
-        (density.at[:, 0, :, 0, :], row),
-        (density.at[:, height - 1, :, SUB - 1, :], last_row),
-        *zip(small, small_out, strict=True),
-    ]
+    small, (plane, *small_out), sems = refs[:6], refs[6:13], refs[13]
+    pieces = [(density.at[0], plane), *zip(small, small_out, strict=True)]
     copies = [pltpu.make_async_copy(a, b, sems.at[i]) for i, (a, b) in enumerate(pieces)]
     for copy in copies:
         copy.start()
@@ -61,26 +55,43 @@
         copy.wait()
 
 
-def hats(values, table, levels):
-    def at(k):
-        return wide(table[k : k + 1, :])
-
-    absorption = [at(0) + at(1) * u for u in values]
-    emission = [at(levels) + at(levels + 1) * u for u in values]
-    for k in range(1, levels - 1):
-        gain_a, gain_e = at(k + 1), at(levels + k + 1)
-        for j, u in enumerate(values):
-            kink = jnp.maximum(u, float(k))
-            absorption[j] = absorption[j] + gain_a * kink
-            emission[j] = emission[j] + gain_e * kink
-    return absorption, emission
-
-
-def interior_kernel(
-    bins, absorb_bins, emit_bins, occupied, row_offsets, col_offsets, density,
-    state, last_state, table, masks, columns, rows, weights, scaled, small,
+def hats(values, table):
+    pieces = table.shape[0] // (2 * (SPAN + 1))
+    results = []
+    for u in values:
+        within = [u >= float(SPAN * i) for i in range(1, pieces)]
+
+        def pick(rows, within=within):
+            chosen = rows[0]
+            for at, row in zip(within, rows[1:], strict=True):
+                chosen = jnp.where(at, row, chosen)
+            return chosen
+
+        t = u - pick([jnp.full((SUB, LANES), float(SPAN * i), F32) for i in range(pieces)])
+        kinks = [t] + [jnp.maximum(t, float(j)) for j in range(1, SPAN)]
+        sums = []
+        for which in range(2):
+
+            def entry(q, which=which):
+                first = which * pieces * (SPAN + 1) + q
+                return pick(
+                    [wide(table[k : k + 1, :]) for k in range(
+                        first, first + pieces * (SPAN + 1), SPAN + 1)]
+                )
+
+            total = entry(0)
+            for j, kink in enumerate(kinks):
+                total = total + entry(j + 1) * kink
+            sums.append(total)
+        results.append(sums)
+    return [r[0] for r in results], [r[1] for r in results]
+
+
+def tables_kernel(
+    bins, absorb_bins, emit_bins, occupied, row_offsets, col_offsets,
+    table, masks, columns, rows, weights, small,
 ):
-    planes, height, tiles = density.shape[:3]
+    height, tiles = weights.shape[1], masks.shape[0]
     levels = bins.shape[1]
     small[...] = jnp.zeros_like(small)
     for i, source in enumerate((bins, absorb_bins, emit_bins, occupied, row_offsets)):
@@ -94,7 +105,6 @@
     columns[1] = jnp.where(ends, 0.0, fraction)
     lane = lax.broadcasted_iota(jnp.int32, (SUB, LANES), 1)
     sub = lax.broadcasted_iota(jnp.int32, (SUB, LANES), 0)
-    lane_end, row_end = lane == LANES - 1, sub == SUB - 1
     bins, absorb_bins, emit_bins, occupied, row_offsets = (
         wide(small[i : i + 1, :]) for i in range(5)
     )
@@ -118,15 +128,36 @@
         masks[t : t + 1, :] = pick(occupied, t)[:1, :]
 
     which = bins.astype(jnp.int32)
-    for first, level, unit in ((0, absorb_bins, -1.0 / math.log(2.0)), (levels, emit_bins, 1.0)):
+    pieces = table.shape[0] // (2 * (SPAN + 1))
+    row = 0
+    for level, unit in ((absorb_bins, -1.0 / math.log(2.0)), (emit_bins, 1.0)):
         value = jnp.take_along_axis(level, which, axis=1, mode="promise_in_bounds") * unit
         slope = pltpu.roll(value, LANES - 1, 1) - value
-        gain = jnp.where(lane == 0, slope, slope - pltpu.roll(slope, 1, 1))
-        shift = jnp.where(lane < levels - 1, gain * lane.astype(F32), 0.0)
-        base = pick(value, 0) - jnp.sum(shift, 1, keepdims=True)
-        table[first : first + 1, :] = base[:1, :]
-        for k in range(levels - 1):
-            table[first + k + 1 : first + k + 2, :] = pick(gain, k)[:1, :]
+        gain = slope - pltpu.roll(slope, 1, 1)
+        base = value
+        for j in range(1, SPAN):
+            base = base - float(j) * pltpu.roll(gain, LANES - j, 1)
+        for i in range(pieces):
+            entries = [(base, 0), (slope, 0)] + [(gain, j) for j in range(1, SPAN)]
+            for vector, j in entries:
+                table[row : row + 1, :] = pick(vector, SPAN * i + j)[:1, :]
+                row += 1
+
+
+def interior_kernel(
+    table, masks, columns, weights, density, state, last_state, row, last_row, scaled, sems
+):
+    planes, height, tiles = density.shape[:3]
+    copies = [
+        pltpu.make_async_copy(density.at[:, 0, :, 0, :], row, sems.at[0]),
+        pltpu.make_async_copy(density.at[:, height - 1, :, SUB - 1, :], last_row, sems.at[1]),
+    ]
+    for copy in copies:
+        copy.start()
+    lane_end = lax.broadcasted_iota(jnp.int32, (SUB, LANES), 1) == LANES - 1
+    row_end = lax.broadcasted_iota(jnp.int32, (SUB, LANES), 0) == SUB - 1
+    near = [weights[0, r] for r in range(height)]
+    far = [weights[1, r] for r in range(height)]
 
     for z in range(planes - 1):
 
@@ -160,7 +191,7 @@
         through = [jnp.ones((SUB, LANES), F32)] * height
         light = [jnp.zeros((SUB, LANES), F32)] * height
         for z in range(planes - 1):
-            absorption, emission = hats([scaled[z, r, t] for r in range(height)], table, levels)
+            absorption, emission = hats([scaled[z, r, t] for r in range(height)], table)
             for r in range(height):
                 total[r] = total[r] + absorption[r] * mask
                 behind = jnp.exp2(total[r])
@@ -172,10 +203,12 @@
         last_state[0, 0, t] = light[-1]
         last_state[1, 0, t] = through[-1]
 
+    for copy in copies:
+        copy.wait()
+
 
 def add_last_plane(density, plane, table, masks, columns, weights, before, state, tiles_of_rows):
     planes, height, tiles = density.shape[:3]
-    levels = table.shape[0] // 2
     some = unless_last("depth")
     lane_end = lax.broadcasted_iota(jnp.int32, (SUB, LANES), 1) == LANES - 1
     row_end = lax.broadcasted_iota(jnp.int32, (SUB, LANES), 0) == SUB - 1
@@ -196,7 +229,7 @@
     group = 4
     count = len(value)
     for first in range(0, count, group):
-        absorption, emission = hats(value[first : first + group], table, levels)
+        absorption, emission = hats(value[first : first + group], table)
         for j, (a, e) in enumerate(zip(absorption, emission, strict=True), first):
             i, t = divmod(j, tiles)
             through = before[1, i, t]
@@ -222,7 +255,6 @@
     density, plane, below, last_row, table, masks, columns, rows, weights, before, state
 ):
     planes, height, tiles = density.shape[:3]
-    levels = table.shape[0] // 2
     add_last_plane(density, plane, table, masks, columns, weights, before, state, [height - 1])
 
     shape = (tiles, LANES)
@@ -242,7 +274,7 @@
     light = jnp.zeros(shape, F32)
     group = 4
     for first in range(0, planes, group):
-        absorption, emission = hats(value[first : first + group], table, levels)
+        absorption, emission = hats(value[first : first + group], table)
         for a, e in zip(absorption, emission, strict=True):
             total = total + a * masks[...]
             behind = jnp.exp2(total)
@@ -293,7 +325,7 @@
 def on_device(density, bin_of_level, absorb_bins, emit_bins, occupancy, col_offsets, row_offsets):
     planes, rows, cols = density.shape
     height, tiles = rows // SUB, cols // LANES
-    levels = bin_of_level.shape[0]
+    pieces = -(-(bin_of_level.shape[0] - 1) // SPAN)
     tiled = density.reshape(planes, height, SUB, tiles, LANES).transpose(0, 1, 3, 2, 4)
     flat = (height, tiles, SUB, LANES)
     upper = (2, height - 1, tiles, SUB, LANES)
@@ -306,36 +338,47 @@
         bin_of_level[None], absorb_bins[None], emit_bins[None], occupancy.reshape(1, tiles),
         row_offsets[None], col_offsets.reshape(tiles, LANES),
     )
-    plane, row, last_row, *small = pl.pallas_call(
+    plane, *small = pl.pallas_call(
         edges_kernel,
         out_shape=[
-            out(*flat), out(planes, tiles, LANES), out(planes, tiles, LANES),
+            out(*flat),
             *[jax.ShapeDtypeStruct(x.shape, x.dtype) for x in small],
         ],
         in_specs=[HBM] * 7,
-        out_specs=[VMEM] * 9,
-        scratch_shapes=[pltpu.SemaphoreType.DMA((9,))],
+        out_specs=[VMEM] * 7,
+        scratch_shapes=[pltpu.SemaphoreType.DMA((7,))],
         compiler_params=params(2),
         name="edges",
     )(*[pltpu.with_memory_space_constraint(x, pltpu.HBM) for x in (tiled, *small)])
     plane = plane_from_behind(plane)
 
     work = density.size
-    above, under, table, masks, columns, last_weights, weights = pl.pallas_call(
+    table, masks, columns, last_weights, weights = pl.pallas_call(
+        tables_kernel,
+        out_shape=[
+            out(2 * (SPAN + 1) * pieces, LANES), out(tiles, LANES), out(2, tiles, LANES), out(2, LANES),
+            out(2, height, SUB, LANES),
+        ],
+        in_specs=[VMEM] * 6,
+        out_specs=[VMEM] * 5,
+        scratch_shapes=[pltpu.VMEM((SUB, LANES), F32)],
+        compiler_params=params(1),
+        name="tables",
+    )(*small)
+    above, under, row, last_row = pl.pallas_call(
         interior_kernel,
         out_shape=[
-            out(*upper), out(*lower), out(2 * levels, LANES), out(tiles, LANES),
-            out(2, tiles, LANES), out(2, LANES), out(2, height, SUB, LANES),
+            out(*upper), out(*lower), out(planes, tiles, LANES), out(planes, tiles, LANES)
         ],
-        in_specs=[VMEM] * 7,
-        out_specs=[VMEM] * 7,
-        scratch_shapes=[pltpu.VMEM((planes - 1, *flat), F32), pltpu.VMEM((SUB, LANES), F32)],
+        in_specs=[VMEM] * 5,
+        out_specs=[VMEM] * 4,
+        scratch_shapes=[pltpu.VMEM((planes - 1, *flat), F32), pltpu.SemaphoreType.DMA((2,))],
         cost_estimate=pl.CostEstimate(
             flops=100 * work, bytes_accessed=4 * work, transcendentals=work
         ),
         compiler_params=params(8),
         name="interior",
-    )(*small, tiled)
+    )(table, masks, columns, weights, tiled)
     above, row = pl.pallas_call(
         upper_kernel,
         out_shape=[out(*upper), out(planes, tiles, LANES)],

time: 28.5 us -> 28.3 us (level)
  starting transfers between devices: 17.7 us -> 19 us
  waiting for transfers between devices: 3.99 us -> 3.17 us
  Pallas kernels: 5.71 us -> 5.05 us
    ppermute x6, starting transfers between devices: 12.7 us -> 14 us  [on_device(): others = [lax.ppermute(state, 'depth', route) for state in states]]
    pallas_call x1, Pallas kernels: 3.36 us -> 2.48 us  [on_device(): pl.pallas_call(interior_kernel, out_shape=[out(*upper), out(*lower), out(...]
    ppermute x6, waiting for transfers between devices: 3.68 us -> 3.17 us  [on_device(): others = [lax.ppermute(state, 'depth', route) for state in states]]
    ppermute x1, waiting for transfers between devices: 0.31 us -> 0.01 us  [from_behind(): return lax.ppermute(block, axis, [((i + 1) % size, i) for i in range(size)])]
    pallas_call x1 -> x2, Pallas kernels: 1.09 us -> 1.38 us  [the longest x1 1 us: on_device(): pl.pallas_call(edges_kernel, out_shape=[out(*flat), *[jax.ShapeDtypeStruc...]
  transfers between devices with their start and end apart: 9 -> 9, of which waited for: 5 -> 2; matrix products, arithmetic and copies ran while one was open for 1% -> 0% of each run, Pallas kernels for 13% -> 11%
where the time goes in v5:
time: 28.3 us; the launch traced here: 28.2 us
  starting transfers between devices  19 us (67%)
  Pallas kernels  5.05 us (18%)
  waiting for transfers between devices  3.17 us (11%)
  between operations  0.79 us (3%)
    ppermute x6, starting transfers between devices, on_device(): others = [lax.ppermute(state, 'depth', route) for state in states]  14 us
    ppermute x1, starting transfers between devices, plane_from_behind(): even = lax.ppermute(plane, 'depth', [(i, i ^ 1) for i in range(depth)])  4.02 us
    ppermute x6, waiting for transfers between devices, on_device(): others = [lax.ppermute(state, 'depth', route) for state in states]  3.17 us
    pallas_call x1, Pallas kernels, on_device(): pl.pallas_call(interior_kernel, out_shape=[out(*upper), out(*lower), out(...  2.48 us
    pallas_call x1, Pallas kernels, on_device(): pl.pallas_call(edges_kernel, out_shape=[out(*flat), *[jax.ShapeDtypeStruc...  1 us
    pallas_call x1, Pallas kernels, on_device(): pl.pallas_call(functools.partial(last_merge_kernel, step=step, parts=part...  0.72 us
  transfers between devices with their start and end apart: 9, of which 2 were waited for; matrix products, arithmetic and copies ran while one was open for 0% of the time, Pallas kernels for 11%

profile of v5, /device:TPU:0, one launch (start us, length us, event | category | flops | bytes accessed | tf_op | source)
XLA Modules:
  0.0 28.2 jit_solution(14571944936358155195)
XLA Ops:
  0.6 0.0 copy-start
  0.6 1.0 %edges.1 = (f32[2,8,8,128]{3,2,1,0:T(8,128)S(1)}, s32[1,16]{1,0:T(1,128)S(1)}, f32[1,8]{1,0:T(1,128)S(1)}, f32[1,8]{1,0:T(1,128)S(1)}, s32[1,8]{1,0:T(1,128)S(1)...) custom-call(f32[16,2,8,8,128]{4,3,2,1,0:T(8,128)} %bitcast.15, s32[1,16]{1,0:T(1,128)} %bitcast.20, f32[1,8]{1,0:T(1,128)} %bitcast.21, ...), custom_call_target="tpu_custom_call" | custom-call | tf_op jit(solution)/shard_map/edges/pallas_call | solution.py:341
  1.6 0.6 %collective-permute-start.1 = (f32[2,8,8,128]{3,2,1,0:T(8,128)S(1)}, f32[2,8,8,128]{3,2,1,0:T(8,128)S(1)}, u32[]{:S(2)}, u32[]{:S(2)}) collective-permute-start(f32[2,8,8,128]{3,2,1,0:T(8,128)S(1)} %get-tuple-element.22), channel_id=1, source_target_pairs={{1,0},{0,1},{3,2},{2,3},{8,4},{9,5},{10,6},{11,7},{4,8},{5,9},{6,1... | collective-permute-start | bytes 196616 | tf_op jit(solution)/shard_map/ppermute | solution.py:35
  2.2 4.0 %collective-permute-start = (f32[2,8,8,128]{3,2,1,0:T(8,128)S(1)}, f32[2,8,8,128]{3,2,1,0:T(8,128)S(1)}, u32[]{:S(2)}, u32[]{:S(2)}) collective-permute-start(f32[2,8,8,128]{3,2,1,0:T(8,128)S(1)} %get-tuple-element.22), channel_id=1, source_target_pairs={{0,4},{4,0},{8,12},{12,8},{16,20},{20,16},{24,28},{28,24},{1,5},{5... | collective-permute-start | bytes 196616 | tf_op jit(solution)/shard_map/ppermute | solution.py:36
  6.2 0.4 %tables.1 = (f32[36,128]{1,0:T(8,128)S(1)}, f32[8,128]{1,0:T(8,128)S(1)}, f32[2,8,128]{2,1,0:T(8,128)S(1)}, f32[2,128]{1,0:T(2,128)S(1)}, f32[2,2,8,128]{3,2,1,0:T(8,128)S(1)}) custom-call(s32[1,16]{1,0:T(1,128)S(1)} %get-tuple-element.23.bins, f32[1,8]{1,0:T(1,128)S(1)} %get-tuple-element.24.absorb_bins, f32[1,8]{1,0:T(1,128)S(1)} %get-tuple-element.25.emit_bins, ...), custom_call_target="tpu_custom_call" | custom-call | tf_op jit(solution)/shard_map/tables/pallas_call | solution.py:356
  6.6 0.0 copy-done
  6.6 2.5 %interior.1 = (f32[2,1,8,8,128]{4,3,2,1,0:T(8,128)S(1)}, f32[2,1,8,8,128]{4,3,2,1,0:T(8,128)S(1)}, f32[16,8,128]{2,1,0:T(8,128)S(1)}, f32[16,8,128]{2,1,0:T(8,128)S(1)}) custom-call(f32[36,128]{1,0:T(8,128)S(1)} %get-tuple-element.29.table, f32[8,128]{1,0:T(8,128)S(1)} %get-tuple-element.30.masks, f32[2,8,128]{2,1,0:T(8,128)S(1)} %get-tuple-element.31.columns, ...), custom_call_target="tpu_custom_call" | custom-call | flops 26214400 | bytes 1048576 | tf_op jit(solution)/shard_map/interior/pallas_call | solution.py:368
  9.1 0.0 collective-permute-done.1
  9.1 0.0 collective-permute-done
  9.1 0.2 upper.1
  9.3 0.5 %collective-permute-start.5 = (f32[16,8,128]{2,1,0:T(8,128)S(1)}, f32[16,8,128]{2,1,0:T(8,128)S(1)}, u32[]{:S(2)}, u32[]{:S(2)}) collective-permute-start(f32[16,8,128]{2,1,0:T(8,128)S(1)} %get-tuple-element.36), channel_id=1, source_target_pairs={{1,0},{2,1},{3,2},{0,3},{5,4},{6,5},{7,6},{4,7},{9,8},{10,9},{11,1... | collective-permute-start | bytes 196616 | tf_op jit(solution)/shard_map/ppermute | solution.py:24
  9.8 2.1 %collective-permute-start.2 = (f32[2,1,8,8,128]{4,3,2,1,0:T(8,128)S(1)}, f32[2,1,8,8,128]{4,3,2,1,0:T(8,128)S(1)}, u32[]{:S(2)}, u32[]{:S(2)}) collective-permute-start(f32[2,1,8,8,128]{4,3,2,1,0:T(8,128)S(1)} %get-tuple-element.35), channel_id=1, source_target_pairs={{0,4},{4,0},{8,12},{12,8},{16,20},{20,16},{24,28},{28,24},{1,5},{5... | collective-permute-start | bytes 196616 | tf_op jit(solution)/shard_map/ppermute | solution.py:409
  11.9 0.0 collective-permute-done.5.below
  11.9 0.3 %lower.1 = f32[2,1,8,8,128]{4,3,2,1,0:T(8,128)S(1)} custom-call(f32[16,2,8,8,128]{4,3,2,1,0:T(8,128)S(1)} %bitcast.18, f32[2,8,8,128]{3,2,1,0:T(8,128)S(1)} %broadcast_select_fusion.plane, f32[16,8,128]{2,1,0:T(8,128)S(1)} %collective-permute-done.5.below, f32[16,8,128]{2,1,0:T(8,128)S(1)} %get-tuple-element.37.last_row, ...), custom_call_target="tpu_custom_call" | custom-call | flops 2621440 | bytes 262144 | tf_op jit(solution)/shard_map/lower/pallas_call | solution.py:391
  12.2 2.0 %collective-permute-start.6 = (f32[2,1,8,8,128]{4,3,2,1,0:T(8,128)S(1)}, f32[2,1,8,8,128]{4,3,2,1,0:T(8,128)S(1)}, u32[]{:S(2)}, u32[]{:S(2)}) collective-permute-start(f32[2,1,8,8,128]{4,3,2,1,0:T(8,128)S(1)} %lower.1), channel_id=1, source_target_pairs={{0,4},{4,0},{8,12},{12,8},{16,20},{20,16},{24,28},{28,24},{1,5},{5... | collective-permute-start | bytes 196616 | tf_op jit(solution)/shard_map/ppermute | solution.py:409
  14.1 0.0 collective-permute-done.2
  14.2 2.1 %collective-permute-start.3 = (f32[2,1,8,8,128]{4,3,2,1,0:T(8,128)S(1)}, f32[2,1,8,8,128]{4,3,2,1,0:T(8,128)S(1)}, u32[]{:S(2)}, u32[]{:S(2)}) collective-permute-start(f32[2,1,8,8,128]{4,3,2,1,0:T(8,128)S(1)} %pad_maximum_fusion), channel_id=1, source_target_pairs={{0,8},{4,12},{8,0},{12,4},{16,24},{20,28},{24,16},{28,20},{1,9},{5... | collective-permute-start | bytes 196616 | tf_op jit(solution)/shard_map/ppermute | solution.py:409
  16.3 0.8 %collective-permute-done.6 = f32[2,1,8,8,128]{4,3,2,1,0:T(8,128)S(1)} collective-permute-done((f32[2,1,8,8,128]{4,3,2,1,0:T(8,128)S(1)}, f32[2,1,8,8,128]{4,3,2,1,0:T(8,128)S(1)}, u32[]{:S(2)}, u32[]{:S(2)}) %collective-permute-start.6) | collective-permute-done | bytes 65568 | tf_op jit(solution)/shard_map/ppermute | solution.py:409
  17.1 2.1 %collective-permute-start.7 = (f32[2,1,8,8,128]{4,3,2,1,0:T(8,128)S(1)}, f32[2,1,8,8,128]{4,3,2,1,0:T(8,128)S(1)}, u32[]{:S(2)}, u32[]{:S(2)}) collective-permute-start(f32[2,1,8,8,128]{4,3,2,1,0:T(8,128)S(1)} %pad_maximum_fusion.2), channel_id=1, source_target_pairs={{0,8},{4,12},{8,0},{12,4},{16,24},{20,28},{24,16},{28,20},{1,9},{5... | collective-permute-start | bytes 196616 | tf_op jit(solution)/shard_map/ppermute | solution.py:409
  19.2 0.0 collective-permute-done.3
  19.3 2.7 %collective-permute-start.4 = (f32[2,1,8,8,128]{4,3,2,1,0:T(8,128)S(1)}, f32[2,1,8,8,128]{4,3,2,1,0:T(8,128)S(1)}, u32[]{:S(2)}, u32[]{:S(2)}) collective-permute-start(f32[2,1,8,8,128]{4,3,2,1,0:T(8,128)S(1)} %pad_maximum_fusion.1.refs_0_), channel_id=1, source_target_pairs={{0,16},{4,20},{8,24},{12,28},{16,0},{20,4},{24,8},{28,12},{1,17},{... | collective-permute-start | bytes 196616 | tf_op jit(solution)/shard_map/ppermute | solution.py:417
  21.9 0.0 collective-permute-done.7
  22.0 3.1 %collective-permute-start.8 = (f32[2,1,8,8,128]{4,3,2,1,0:T(8,128)S(1)}, f32[2,1,8,8,128]{4,3,2,1,0:T(8,128)S(1)}, u32[]{:S(2)}, u32[]{:S(2)}) collective-permute-start(f32[2,1,8,8,128]{4,3,2,1,0:T(8,128)S(1)} %pad_maximum_fusion.3.refs_3_), channel_id=1, source_target_pairs={{0,16},{4,20},{8,24},{12,28},{16,0},{20,4},{24,8},{28,12},{1,17},{... | collective-permute-start | bytes 196616 | tf_op jit(solution)/shard_map/ppermute | solution.py:417
  25.1 0.0 collective-permute-done.4.refs_1_
  25.1 2.4 %collective-permute-done.8.refs_4_ = f32[2,1,8,8,128]{4,3,2,1,0:T(8,128)S(1)} collective-permute-done((f32[2,1,8,8,128]{4,3,2,1,0:T(8,128)S(1)}, f32[2,1,8,8,128]{4,3,2,1,0:T(8,128)S(1)}, u32[]{:S(2)}, u32[]{:S(2)}) %collective-permute-start.8) | collective-permute-done | bytes 65568 | tf_op jit(solution)/shard_map/ppermute | solution.py:417
  27.5 0.7 %last_merge.1 = (f32[1,2,8,8,128]{4,3,2,1,0:T(8,128)}, f32[2,2,8,8,128]{4,3,2,1,0:T(8,128)}) custom-call(f32[2,1,8,8,128]{4,3,2,1,0:T(8,128)S(1)} %pad_maximum_fusion.1.refs_0_, f32[2,1,8,8,128]{4,3,2,1,0:T(8,128)S(1)} %collective-permute-done.4.refs_1_, f32[1,1,8,8,128]{4,3,2,1,0:T(8,128)S(1)} %fusion.3.refs_2_, ...), custom_call_target="tpu_custom_call" | custom-call | tf_op jit(solution)/shard_map/last_merge/pallas_call | solution.py:419
  (15 shorter events, 0.1 us)
Async XLA Ops:
  0.6 6.0 %copy-start = (f32[16,16,1024]{2,1,0:T(8,128)S(1)}, f32[16,16,1024]{2,1,0:T(8,128)}, u32[]{:S(2)}) copy-start(f32[16,16,1024]{2,1,0:T(8,128)} %param.7) | copy-start | bytes 3145732
  1.6 7.5 %collective-permute-start.1 = (f32[2,8,8,128]{3,2,1,0:T(8,128)S(1)}, f32[2,8,8,128]{3,2,1,0:T(8,128)S(1)}, u32[]{:S(2)}, u32[]{:S(2)}) collective-permute-start(f32[2,8,8,128]{3,2,1,0:T(8,128)S(1)} %get-tuple-element.22), channel_id=1, source_target_pairs={{1,0},{0,1},{3,2},{2,3},{8,4},{9,5},{10,6},{11,7},{4,8},{5,9},{6,1... | collective-permute-start | bytes 196616 | tf_op jit(solution)/shard_map/ppermute | solution.py:35
  2.2 6.9 %collective-permute-start = (f32[2,8,8,128]{3,2,1,0:T(8,128)S(1)}, f32[2,8,8,128]{3,2,1,0:T(8,128)S(1)}, u32[]{:S(2)}, u32[]{:S(2)}) collective-permute-start(f32[2,8,8,128]{3,2,1,0:T(8,128)S(1)} %get-tuple-element.22), channel_id=1, source_target_pairs={{0,4},{4,0},{8,12},{12,8},{16,20},{20,16},{24,28},{28,24},{1,5},{5... | collective-permute-start | bytes 196616 | tf_op jit(solution)/shard_map/ppermute | solution.py:36
  9.3 2.5 %collective-permute-start.5 = (f32[16,8,128]{2,1,0:T(8,128)S(1)}, f32[16,8,128]{2,1,0:T(8,128)S(1)}, u32[]{:S(2)}, u32[]{:S(2)}) collective-permute-start(f32[16,8,128]{2,1,0:T(8,128)S(1)} %get-tuple-element.36), channel_id=1, source_target_pairs={{1,0},{2,1},{3,2},{0,3},{5,4},{6,5},{7,6},{4,7},{9,8},{10,9},{11,1... | collective-permute-start | bytes 196616 | tf_op jit(solution)/shard_map/ppermute | solution.py:24
  9.8 4.4 %collective-permute-start.2 = (f32[2,1,8,8,128]{4,3,2,1,0:T(8,128)S(1)}, f32[2,1,8,8,128]{4,3,2,1,0:T(8,128)S(1)}, u32[]{:S(2)}, u32[]{:S(2)}) collective-permute-start(f32[2,1,8,8,128]{4,3,2,1,0:T(8,128)S(1)} %get-tuple-element.35), channel_id=1, source_target_pairs={{0,4},{4,0},{8,12},{12,8},{16,20},{20,16},{24,28},{28,24},{1,5},{5... | collective-permute-start | bytes 196616 | tf_op jit(solution)/shard_map/ppermute | solution.py:409
  12.2 4.9 %collective-permute-start.6 = (f32[2,1,8,8,128]{4,3,2,1,0:T(8,128)S(1)}, f32[2,1,8,8,128]{4,3,2,1,0:T(8,128)S(1)}, u32[]{:S(2)}, u32[]{:S(2)}) collective-permute-start(f32[2,1,8,8,128]{4,3,2,1,0:T(8,128)S(1)} %lower.1), channel_id=1, source_target_pairs={{0,4},{4,0},{8,12},{12,8},{16,20},{20,16},{24,28},{28,24},{1,5},{5... | collective-permute-start | bytes 196616 | tf_op jit(solution)/shard_map/ppermute | solution.py:409
  14.2 5.0 %collective-permute-start.3 = (f32[2,1,8,8,128]{4,3,2,1,0:T(8,128)S(1)}, f32[2,1,8,8,128]{4,3,2,1,0:T(8,128)S(1)}, u32[]{:S(2)}, u32[]{:S(2)}) collective-permute-start(f32[2,1,8,8,128]{4,3,2,1,0:T(8,128)S(1)} %pad_maximum_fusion), channel_id=1, source_target_pairs={{0,8},{4,12},{8,0},{12,4},{16,24},{20,28},{24,16},{28,20},{1,9},{5... | collective-permute-start | bytes 196616 | tf_op jit(solution)/shard_map/ppermute | solution.py:409
  17.1 4.8 %collective-permute-start.7 = (f32[2,1,8,8,128]{4,3,2,1,0:T(8,128)S(1)}, f32[2,1,8,8,128]{4,3,2,1,0:T(8,128)S(1)}, u32[]{:S(2)}, u32[]{:S(2)}) collective-permute-start(f32[2,1,8,8,128]{4,3,2,1,0:T(8,128)S(1)} %pad_maximum_fusion.2), channel_id=1, source_target_pairs={{0,8},{4,12},{8,0},{12,4},{16,24},{20,28},{24,16},{28,20},{1,9},{5... | collective-permute-start | bytes 196616 | tf_op jit(solution)/shard_map/ppermute | solution.py:409
  19.3 5.8 %collective-permute-start.4 = (f32[2,1,8,8,128]{4,3,2,1,0:T(8,128)S(1)}, f32[2,1,8,8,128]{4,3,2,1,0:T(8,128)S(1)}, u32[]{:S(2)}, u32[]{:S(2)}) collective-permute-start(f32[2,1,8,8,128]{4,3,2,1,0:T(8,128)S(1)} %pad_maximum_fusion.1.refs_0_), channel_id=1, source_target_pairs={{0,16},{4,20},{8,24},{12,28},{16,0},{20,4},{24,8},{28,12},{1,17},{... | collective-permute-start | bytes 196616 | tf_op jit(solution)/shard_map/ppermute | solution.py:417
  22.0 5.5 %collective-permute-start.8 = (f32[2,1,8,8,128]{4,3,2,1,0:T(8,128)S(1)}, f32[2,1,8,8,128]{4,3,2,1,0:T(8,128)S(1)}, u32[]{:S(2)}, u32[]{:S(2)}) collective-permute-start(f32[2,1,8,8,128]{4,3,2,1,0:T(8,128)S(1)} %pad_maximum_fusion.3.refs_3_), channel_id=1, source_target_pairs={{0,16},{4,20},{8,24},{12,28},{16,0},{20,4},{24,8},{28,12},{1,17},{... | collective-permute-start | bytes 196616 | tf_op jit(solution)/shard_map/ppermute | solution.py:417

commit v6 on v5

--- a/solution.py
+++ b/solution.py
@@ -238,25 +238,27 @@
             state[1, i, t] = behind
 
 
-def upper_kernel(
-    density, plane, row, table, masks, columns, weights, before, state, row_sums
-):
-    planes, height, tiles = density.shape[:3]
+def row_sums_kernel(plane, row, row_sums):
+    planes, tiles = row.shape[:2]
     for z in range(planes - 1):
         row_sums[z] = row[z] + row[z + 1]
     after = jnp.concatenate([plane[0, t, :1, :] for t in range(tiles)], 0)
     row_sums[planes - 1] = row[planes - 1] + unless_last("depth") * after
-    add_last_plane(
-        density, plane, table, masks, columns, weights, before, state, range(height - 1)
-    )
-
-
-def lower_kernel(
-    density, plane, below, last_row, table, masks, columns, rows, weights, before, state
+
+
+def last_plane_kernel(
+    density, plane, table, masks, columns, weights, above, under, above_out, under_out
 ):
-    planes, height, tiles = density.shape[:3]
-    add_last_plane(density, plane, table, masks, columns, weights, before, state, [height - 1])
-
+    height = density.shape[1]
+    args = (density, plane, table, masks, columns, weights)
+    add_last_plane(*args, above, above_out, range(height - 1))
+    add_last_plane(*args, under, under_out, [height - 1])
+
+
+def last_row_kernel(plane, below, last_row, table, masks, columns, rows, before, state):
+    height, tiles = plane.shape[:2]
+    planes = below.shape[0]
+    state[...] = before[...]
     shape = (tiles, LANES)
     fold_end = lax.broadcasted_iota(jnp.int32, shape, 1) == LANES - 1
     near, far = rows[0:1, :], unless_last("rows") * rows[1:2, :]
@@ -379,26 +381,37 @@
         compiler_params=params(8),
         name="interior",
     )(table, masks, columns, weights, tiled)
-    above, row = pl.pallas_call(
-        upper_kernel,
-        out_shape=[out(*upper), out(planes, tiles, LANES)],
+    row = pl.pallas_call(
+        row_sums_kernel,
+        out_shape=out(planes, tiles, LANES),
+        in_specs=[VMEM] * 2,
+        out_specs=VMEM,
+        compiler_params=params(1),
+        name="row_sums",
+    )(plane, row)
+    row = from_behind(row, "rows")
+    above, under = pl.pallas_call(
+        last_plane_kernel,
+        out_shape=[out(*upper), out(*lower)],
         in_specs=[VMEM] * 8,
         out_specs=[VMEM] * 2,
+        cost_estimate=pl.CostEstimate(
+            flops=10 * work, bytes_accessed=work, transcendentals=work // 8
+        ),
         compiler_params=params(8),
-        name="upper",
-    )(tiled, plane, row, table, masks, columns, weights, above)
-    row = from_behind(row, "rows")
+        name="last_plane",
+    )(tiled, plane, table, masks, columns, weights, above, under)
     under = pl.pallas_call(
-        lower_kernel,
+        last_row_kernel,
         out_shape=out(*lower),
-        in_specs=[VMEM] * 10,
+        in_specs=[VMEM] * 8,
         out_specs=VMEM,
         cost_estimate=pl.CostEstimate(
             flops=10 * work, bytes_accessed=work, transcendentals=work // 8
         ),
         compiler_params=params(8),
-        name="lower",
-    )(tiled, plane, row, last_row, table, masks, columns, last_weights, weights, under)
+        name="last_row",
+    )(plane, row, last_row, table, masks, columns, last_weights, under)
 
     size = lax.axis_size("depth")
     states = [above, under]

time: 28.3 us -> 28.4 us (level)
  waiting for transfers between devices: 3.17 us -> 3.69 us
  starting transfers between devices: 19 us -> 18.6 us
    ppermute x6, waiting for transfers between devices: 3.17 us -> 3.68 us  [on_device(): others = [lax.ppermute(state, 'depth', route) for state in states]]
    ppermute x6, starting transfers between devices: 14 us -> 13.6 us  [on_device(): others = [lax.ppermute(state, 'depth', route) for state in states]]
  transfers between devices with their start and end apart: 9 -> 9, of which waited for: 2 -> 3; matrix products, arithmetic and copies ran while one was open for 0% -> 1% of each run, Pallas kernels for 11% -> 12%
where the time goes in v6:
time: 28.4 us; the launch traced here: 28.3 us
  starting transfers between devices  18.6 us (65%)
  Pallas kernels  5.06 us (18%)
  waiting for transfers between devices  3.69 us (13%)
  between operations  0.79 us (3%)
    ppermute x6, starting transfers between devices, on_device(): others = [lax.ppermute(state, 'depth', route) for state in states]  13.6 us
    ppermute x1, starting transfers between devices, plane_from_behind(): even = lax.ppermute(plane, 'depth', [(i, i ^ 1) for i in range(depth)])  4.02 us
    ppermute x6, waiting for transfers between devices, on_device(): others = [lax.ppermute(state, 'depth', route) for state in states]  3.68 us
    pallas_call x1, Pallas kernels, on_device(): pl.pallas_call(interior_kernel, out_shape=[out(*upper), out(*lower), out(...  2.48 us
    pallas_call x1, Pallas kernels, on_device(): pl.pallas_call(edges_kernel, out_shape=[out(*flat), *[jax.ShapeDtypeStruc...  1 us
    pallas_call x1, Pallas kernels, on_device(): pl.pallas_call(functools.partial(last_merge_kernel, step=step, parts=part...  0.72 us
  transfers between devices with their start and end apart: 9, of which 3 were waited for; matrix products, arithmetic and copies ran while one was open for 1% of the time, Pallas kernels for 12%

profile of v6, /device:TPU:0, one launch (start us, length us, event | category | flops | bytes accessed | tf_op | source)
XLA Modules:
  0.0 28.3 jit_solution(12277672110030921619)
XLA Ops:
  0.6 0.0 copy-start
  0.6 1.0 %edges.1 = (f32[2,8,8,128]{3,2,1,0:T(8,128)S(1)}, s32[1,16]{1,0:T(1,128)S(1)}, f32[1,8]{1,0:T(1,128)S(1)}, f32[1,8]{1,0:T(1,128)S(1)}, s32[1,8]{1,0:T(1,128)S(1)...) custom-call(f32[16,2,8,8,128]{4,3,2,1,0:T(8,128)} %bitcast.15, s32[1,16]{1,0:T(1,128)} %bitcast.19, f32[1,8]{1,0:T(1,128)} %bitcast.20, ...), custom_call_target="tpu_custom_call" | custom-call | tf_op jit(solution)/shard_map/edges/pallas_call | solution.py:343
  1.6 0.6 %collective-permute-start.1 = (f32[2,8,8,128]{3,2,1,0:T(8,128)S(1)}, f32[2,8,8,128]{3,2,1,0:T(8,128)S(1)}, u32[]{:S(2)}, u32[]{:S(2)}) collective-permute-start(f32[2,8,8,128]{3,2,1,0:T(8,128)S(1)} %get-tuple-element.22), channel_id=1, source_target_pairs={{1,0},{0,1},{3,2},{2,3},{8,4},{9,5},{10,6},{11,7},{4,8},{5,9},{6,1... | collective-permute-start | bytes 196616 | tf_op jit(solution)/shard_map/ppermute | solution.py:35
  2.2 4.0 %collective-permute-start = (f32[2,8,8,128]{3,2,1,0:T(8,128)S(1)}, f32[2,8,8,128]{3,2,1,0:T(8,128)S(1)}, u32[]{:S(2)}, u32[]{:S(2)}) collective-permute-start(f32[2,8,8,128]{3,2,1,0:T(8,128)S(1)} %get-tuple-element.22), channel_id=1, source_target_pairs={{0,4},{4,0},{8,12},{12,8},{16,20},{20,16},{24,28},{28,24},{1,5},{5... | collective-permute-start | bytes 196616 | tf_op jit(solution)/shard_map/ppermute | solution.py:36
  6.2 0.4 %tables.1 = (f32[36,128]{1,0:T(8,128)S(1)}, f32[8,128]{1,0:T(8,128)S(1)}, f32[2,8,128]{2,1,0:T(8,128)S(1)}, f32[2,128]{1,0:T(2,128)S(1)}, f32[2,2,8,128]{3,2,1,0:T(8,128)S(1)}) custom-call(s32[1,16]{1,0:T(1,128)S(1)} %get-tuple-element.23.bins, f32[1,8]{1,0:T(1,128)S(1)} %get-tuple-element.24.absorb_bins, f32[1,8]{1,0:T(1,128)S(1)} %get-tuple-element.25.emit_bins, ...), custom_call_target="tpu_custom_call" | custom-call | tf_op jit(solution)/shard_map/tables/pallas_call | solution.py:358
  6.6 0.0 copy-done
  6.6 2.5 %interior.1 = (f32[2,1,8,8,128]{4,3,2,1,0:T(8,128)S(1)}, f32[2,1,8,8,128]{4,3,2,1,0:T(8,128)S(1)}, f32[16,8,128]{2,1,0:T(8,128)S(1)}, f32[16,8,128]{2,1,0:T(8,128)S(1)}) custom-call(f32[36,128]{1,0:T(8,128)S(1)} %get-tuple-element.29.table, f32[8,128]{1,0:T(8,128)S(1)} %get-tuple-element.30.masks, f32[2,8,128]{2,1,0:T(8,128)S(1)} %get-tuple-element.31.columns, ...), custom_call_target="tpu_custom_call" | custom-call | flops 26214400 | bytes 1048576 | tf_op jit(solution)/shard_map/interior/pallas_call | solution.py:370
  9.1 0.0 collective-permute-done.1
  9.1 0.0 collective-permute-done
  9.2 0.5 %collective-permute-start.5 = (f32[16,8,128]{2,1,0:T(8,128)S(1)}, f32[16,8,128]{2,1,0:T(8,128)S(1)}, u32[]{:S(2)}, u32[]{:S(2)}) collective-permute-start(f32[16,8,128]{2,1,0:T(8,128)S(1)} %row_sums.1), channel_id=1, source_target_pairs={{1,0},{2,1},{3,2},{0,3},{5,4},{6,5},{7,6},{4,7},{9,8},{10,9},{11,1... | collective-permute-start | bytes 196616 | tf_op jit(solution)/shard_map/ppermute | solution.py:24
  9.6 0.2 last_plane.1
  9.8 2.2 %collective-permute-start.2 = (f32[2,1,8,8,128]{4,3,2,1,0:T(8,128)S(1)}, f32[2,1,8,8,128]{4,3,2,1,0:T(8,128)S(1)}, u32[]{:S(2)}, u32[]{:S(2)}) collective-permute-start(f32[2,1,8,8,128]{4,3,2,1,0:T(8,128)S(1)} %get-tuple-element.35), channel_id=1, source_target_pairs={{0,4},{4,0},{8,12},{12,8},{16,20},{20,16},{24,28},{28,24},{1,5},{5... | collective-permute-start | bytes 196616 | tf_op jit(solution)/shard_map/ppermute | solution.py:422
  12.0 0.0 collective-permute-done.5.below
  12.0 0.2 last_row.1
  12.2 1.7 %collective-permute-start.6 = (f32[2,1,8,8,128]{4,3,2,1,0:T(8,128)S(1)}, f32[2,1,8,8,128]{4,3,2,1,0:T(8,128)S(1)}, u32[]{:S(2)}, u32[]{:S(2)}) collective-permute-start(f32[2,1,8,8,128]{4,3,2,1,0:T(8,128)S(1)} %last_row.1), channel_id=1, source_target_pairs={{0,4},{4,0},{8,12},{12,8},{16,20},{20,16},{24,28},{28,24},{1,5},{5... | collective-permute-start | bytes 196616 | tf_op jit(solution)/shard_map/ppermute | solution.py:422
  13.9 0.3 %collective-permute-done.2 = f32[2,1,8,8,128]{4,3,2,1,0:T(8,128)S(1)} collective-permute-done((f32[2,1,8,8,128]{4,3,2,1,0:T(8,128)S(1)}, f32[2,1,8,8,128]{4,3,2,1,0:T(8,128)S(1)}, u32[]{:S(2)}, u32[]{:S(2)}) %collective-permute-start.2) | collective-permute-done | bytes 65568 | tf_op jit(solution)/shard_map/ppermute | solution.py:422
  14.3 2.2 %collective-permute-start.3 = (f32[2,1,8,8,128]{4,3,2,1,0:T(8,128)S(1)}, f32[2,1,8,8,128]{4,3,2,1,0:T(8,128)S(1)}, u32[]{:S(2)}, u32[]{:S(2)}) collective-permute-start(f32[2,1,8,8,128]{4,3,2,1,0:T(8,128)S(1)} %pad_maximum_fusion), channel_id=1, source_target_pairs={{0,8},{4,12},{8,0},{12,4},{16,24},{20,28},{24,16},{28,20},{1,9},{5... | collective-permute-start | bytes 196616 | tf_op jit(solution)/shard_map/ppermute | solution.py:422
  16.5 0.6 %collective-permute-done.6 = f32[2,1,8,8,128]{4,3,2,1,0:T(8,128)S(1)} collective-permute-done((f32[2,1,8,8,128]{4,3,2,1,0:T(8,128)S(1)}, f32[2,1,8,8,128]{4,3,2,1,0:T(8,128)S(1)}, u32[]{:S(2)}, u32[]{:S(2)}) %collective-permute-start.6) | collective-permute-done | bytes 65568 | tf_op jit(solution)/shard_map/ppermute | solution.py:422
  17.2 1.8 %collective-permute-start.7 = (f32[2,1,8,8,128]{4,3,2,1,0:T(8,128)S(1)}, f32[2,1,8,8,128]{4,3,2,1,0:T(8,128)S(1)}, u32[]{:S(2)}, u32[]{:S(2)}) collective-permute-start(f32[2,1,8,8,128]{4,3,2,1,0:T(8,128)S(1)} %pad_maximum_fusion.2), channel_id=1, source_target_pairs={{0,8},{4,12},{8,0},{12,4},{16,24},{20,28},{24,16},{28,20},{1,9},{5... | collective-permute-start | bytes 196616 | tf_op jit(solution)/shard_map/ppermute | solution.py:422
  19.0 0.0 collective-permute-done.3
  19.0 2.8 %collective-permute-start.4 = (f32[2,1,8,8,128]{4,3,2,1,0:T(8,128)S(1)}, f32[2,1,8,8,128]{4,3,2,1,0:T(8,128)S(1)}, u32[]{:S(2)}, u32[]{:S(2)}) collective-permute-start(f32[2,1,8,8,128]{4,3,2,1,0:T(8,128)S(1)} %pad_maximum_fusion.1.refs_0_), channel_id=1, source_target_pairs={{0,16},{4,20},{8,24},{12,28},{16,0},{20,4},{24,8},{28,12},{1,17},{... | collective-permute-start | bytes 196616 | tf_op jit(solution)/shard_map/ppermute | solution.py:430
  21.9 0.0 collective-permute-done.7
  21.9 2.9 %collective-permute-start.8 = (f32[2,1,8,8,128]{4,3,2,1,0:T(8,128)S(1)}, f32[2,1,8,8,128]{4,3,2,1,0:T(8,128)S(1)}, u32[]{:S(2)}, u32[]{:S(2)}) collective-permute-start(f32[2,1,8,8,128]{4,3,2,1,0:T(8,128)S(1)} %pad_maximum_fusion.3.refs_3_), channel_id=1, source_target_pairs={{0,16},{4,20},{8,24},{12,28},{16,0},{20,4},{24,8},{28,12},{1,17},{... | collective-permute-start | bytes 196616 | tf_op jit(solution)/shard_map/ppermute | solution.py:430
  24.8 0.0 collective-permute-done.4.refs_1_
  24.9 2.7 %collective-permute-done.8.refs_4_ = f32[2,1,8,8,128]{4,3,2,1,0:T(8,128)S(1)} collective-permute-done((f32[2,1,8,8,128]{4,3,2,1,0:T(8,128)S(1)}, f32[2,1,8,8,128]{4,3,2,1,0:T(8,128)S(1)}, u32[]{:S(2)}, u32[]{:S(2)}) %collective-permute-start.8) | collective-permute-done | bytes 65568 | tf_op jit(solution)/shard_map/ppermute | solution.py:430
  27.6 0.7 %last_merge.1 = (f32[1,2,8,8,128]{4,3,2,1,0:T(8,128)}, f32[2,2,8,8,128]{4,3,2,1,0:T(8,128)}) custom-call(f32[2,1,8,8,128]{4,3,2,1,0:T(8,128)S(1)} %pad_maximum_fusion.1.refs_0_, f32[2,1,8,8,128]{4,3,2,1,0:T(8,128)S(1)} %collective-permute-done.4.refs_1_, f32[1,1,8,8,128]{4,3,2,1,0:T(8,128)S(1)} %fusion.3.refs_2_, ...), custom_call_target="tpu_custom_call" | custom-call | tf_op jit(solution)/shard_map/last_merge/pallas_call | solution.py:432
  (16 shorter events, 0.2 us)
Async XLA Ops:
  0.6 6.0 %copy-start = (f32[16,16,1024]{2,1,0:T(8,128)S(1)}, f32[16,16,1024]{2,1,0:T(8,128)}, u32[]{:S(2)}) copy-start(f32[16,16,1024]{2,1,0:T(8,128)} %param.7) | copy-start | bytes 3145732
  1.6 7.5 %collective-permute-start.1 = (f32[2,8,8,128]{3,2,1,0:T(8,128)S(1)}, f32[2,8,8,128]{3,2,1,0:T(8,128)S(1)}, u32[]{:S(2)}, u32[]{:S(2)}) collective-permute-start(f32[2,8,8,128]{3,2,1,0:T(8,128)S(1)} %get-tuple-element.22), channel_id=1, source_target_pairs={{1,0},{0,1},{3,2},{2,3},{8,4},{9,5},{10,6},{11,7},{4,8},{5,9},{6,1... | collective-permute-start | bytes 196616 | tf_op jit(solution)/shard_map/ppermute | solution.py:35
  2.2 6.9 %collective-permute-start = (f32[2,8,8,128]{3,2,1,0:T(8,128)S(1)}, f32[2,8,8,128]{3,2,1,0:T(8,128)S(1)}, u32[]{:S(2)}, u32[]{:S(2)}) collective-permute-start(f32[2,8,8,128]{3,2,1,0:T(8,128)S(1)} %get-tuple-element.22), channel_id=1, source_target_pairs={{0,4},{4,0},{8,12},{12,8},{16,20},{20,16},{24,28},{28,24},{1,5},{5... | collective-permute-start | bytes 196616 | tf_op jit(solution)/shard_map/ppermute | solution.py:36
  9.2 2.8 %collective-permute-start.5 = (f32[16,8,128]{2,1,0:T(8,128)S(1)}, f32[16,8,128]{2,1,0:T(8,128)S(1)}, u32[]{:S(2)}, u32[]{:S(2)}) collective-permute-start(f32[16,8,128]{2,1,0:T(8,128)S(1)} %row_sums.1), channel_id=1, source_target_pairs={{1,0},{2,1},{3,2},{0,3},{5,4},{6,5},{7,6},{4,7},{9,8},{10,9},{11,1... | collective-permute-start | bytes 196616 | tf_op jit(solution)/shard_map/ppermute | solution.py:24
  9.8 4.4 %collective-permute-start.2 = (f32[2,1,8,8,128]{4,3,2,1,0:T(8,128)S(1)}, f32[2,1,8,8,128]{4,3,2,1,0:T(8,128)S(1)}, u32[]{:S(2)}, u32[]{:S(2)}) collective-permute-start(f32[2,1,8,8,128]{4,3,2,1,0:T(8,128)S(1)} %get-tuple-element.35), channel_id=1, source_target_pairs={{0,4},{4,0},{8,12},{12,8},{16,20},{20,16},{24,28},{28,24},{1,5},{5... | collective-permute-start | bytes 196616 | tf_op jit(solution)/shard_map/ppermute | solution.py:422
  12.2 4.9 %collective-permute-start.6 = (f32[2,1,8,8,128]{4,3,2,1,0:T(8,128)S(1)}, f32[2,1,8,8,128]{4,3,2,1,0:T(8,128)S(1)}, u32[]{:S(2)}, u32[]{:S(2)}) collective-permute-start(f32[2,1,8,8,128]{4,3,2,1,0:T(8,128)S(1)} %last_row.1), channel_id=1, source_target_pairs={{0,4},{4,0},{8,12},{12,8},{16,20},{20,16},{24,28},{28,24},{1,5},{5... | collective-permute-start | bytes 196616 | tf_op jit(solution)/shard_map/ppermute | solution.py:422
  14.3 4.7 %collective-permute-start.3 = (f32[2,1,8,8,128]{4,3,2,1,0:T(8,128)S(1)}, f32[2,1,8,8,128]{4,3,2,1,0:T(8,128)S(1)}, u32[]{:S(2)}, u32[]{:S(2)}) collective-permute-start(f32[2,1,8,8,128]{4,3,2,1,0:T(8,128)S(1)} %pad_maximum_fusion), channel_id=1, source_target_pairs={{0,8},{4,12},{8,0},{12,4},{16,24},{20,28},{24,16},{28,20},{1,9},{5... | collective-permute-start | bytes 196616 | tf_op jit(solution)/shard_map/ppermute | solution.py:422
  17.2 4.7 %collective-permute-start.7 = (f32[2,1,8,8,128]{4,3,2,1,0:T(8,128)S(1)}, f32[2,1,8,8,128]{4,3,2,1,0:T(8,128)S(1)}, u32[]{:S(2)}, u32[]{:S(2)}) collective-permute-start(f32[2,1,8,8,128]{4,3,2,1,0:T(8,128)S(1)} %pad_maximum_fusion.2), channel_id=1, source_target_pairs={{0,8},{4,12},{8,0},{12,4},{16,24},{20,28},{24,16},{28,20},{1,9},{5... | collective-permute-start | bytes 196616 | tf_op jit(solution)/shard_map/ppermute | solution.py:422
  19.0 5.8 %collective-permute-start.4 = (f32[2,1,8,8,128]{4,3,2,1,0:T(8,128)S(1)}, f32[2,1,8,8,128]{4,3,2,1,0:T(8,128)S(1)}, u32[]{:S(2)}, u32[]{:S(2)}) collective-permute-start(f32[2,1,8,8,128]{4,3,2,1,0:T(8,128)S(1)} %pad_maximum_fusion.1.refs_0_), channel_id=1, source_target_pairs={{0,16},{4,20},{8,24},{12,28},{16,0},{20,4},{24,8},{28,12},{1,17},{... | collective-permute-start | bytes 196616 | tf_op jit(solution)/shard_map/ppermute | solution.py:430
  21.9 5.6 %collective-permute-start.8 = (f32[2,1,8,8,128]{4,3,2,1,0:T(8,128)S(1)}, f32[2,1,8,8,128]{4,3,2,1,0:T(8,128)S(1)}, u32[]{:S(2)}, u32[]{:S(2)}) collective-permute-start(f32[2,1,8,8,128]{4,3,2,1,0:T(8,128)S(1)} %pad_maximum_fusion.3.refs_3_), channel_id=1, source_target_pairs={{0,16},{4,20},{8,24},{12,28},{16,0},{20,4},{24,8},{28,12},{1,17},{... | collective-permute-start | bytes 196616 | tf_op jit(solution)/shard_map/ppermute | solution.py:430
